TPU v7x, 32 devices: a whole 2x2x4 slice. The times are simulated.
32 devices in a mesh: pb: 8 (over z, x), ka: 4 (over y, core).
Axes of the slice: x: 2, y: 2, z: 4, core: 2. Of those that a mesh axis runs over, the one named last changes fastest.
Arguments:
- query_saved: bfloat16 [1024, 1024], P(('pb', 'ka')), may hold values from -6 to 6
- key_saved: bfloat16 [2048, 1024], P(('ka', 'pb')), may hold values from -6 to 6
- value_saved: bfloat16 [2048, 1024], P(('ka', 'pb')), may hold values from -6 to 6
- out_grad: bfloat16 [1024, 1024], P(('pb', 'ka')), may hold values from -768 to 768
- log_norm: bfloat16 [16, 1024], P(None, ('pb', 'ka')), as said below
- row_delta: bfloat16 [16, 1024], P(None, ('pb', 'ka')), may hold values from -1536 to 1536
- weight_query: bfloat16 [1024, 1024], replicated, may hold values from -0.1875 to 0.1875
- weight_key: bfloat16 [1024, 1024], replicated, may hold values from -0.1875 to 0.1875
- weight_value: bfloat16 [1024, 1024], replicated, may hold values from -0.1875 to 0.1875
Outputs:
- dx_query: bfloat16 [1024, 1024], P(('pb', 'ka'))
- dx_keyvalue: bfloat16 [2048, 1024], P(('ka', 'pb'))
Inputs may be any that keep to these rules, and one draw needn't show every extreme that they name: `log_norm`: each entry lies within 2 of 0.5 plus the natural logarithm of 2048.
All inputs are finite; a program needn't handle non-finite values.
Results may differ from a plain program's by a relative error of at most 0.008.
Values may be sent and summed in bfloat16 or wider, within the bound.
No kernel may reach another device: no remote copies, remote signals or barrier semaphores. Data moves between devices by JAX's collectives and lax.ppermute only.
A program may use at most 128 MiB of HBM per device.

v0:
```python
import jax
import jax.numpy as jnp
from jax import lax
from jax.sharding import PartitionSpec as P

HEAD_DIM = 64


def project(grads, weights):
    contract = (((1,), (1,)), ((), ()))
    upper = grads.astype(jnp.bfloat16)
    lower = (grads - upper.astype(jnp.float32)).astype(jnp.bfloat16)
    first = lax.dot_general(upper, weights, contract, preferred_element_type=jnp.float32)
    return first + lax.dot_general(lower, weights, contract, preferred_element_type=jnp.float32)


def local(
    query_saved,
    key_saved,
    value_saved,
    out_grad,
    log_norm,
    row_delta,
    weight_query,
    weight_key,
    weight_value,
):
    query_block, grad_out_block, norm_block, delta_block = (
        lax.all_gather(query_saved, "ka", axis=0, tiled=True),
        lax.all_gather(out_grad, "ka", axis=0, tiled=True),
        lax.all_gather(log_norm, "ka", axis=1, tiled=True),
        lax.all_gather(row_delta, "ka", axis=1, tiled=True),
    )
    key_block, value_block = (
        lax.all_gather(key_saved, "pb", axis=0, tiled=True),
        lax.all_gather(value_saved, "pb", axis=0, tiled=True),
    )
    query_rows = query_block.shape[0]
    key_rows = key_block.shape[0]
    model_width = query_block.shape[1]
    pair_width = 2 * HEAD_DIM
    pair_count = model_width // pair_width
    score_scale = 1.0 / HEAD_DIM**0.5

    def columns(source, row_count, column):
        return lax.dynamic_slice_in_dim(source, column, pair_width, 1).reshape(
            row_count, 2, HEAD_DIM
        )

    def head_pair(pair_index, totals):
        grad_query, grad_key, grad_value = totals
        column = pair_index * pair_width
        queries = columns(query_block, query_rows, column)
        grads_out = columns(grad_out_block, query_rows, column)
        keys_pair = columns(key_block, key_rows, column)
        values_pair = columns(value_block, key_rows, column)
        norm_pair = lax.dynamic_slice_in_dim(norm_block, pair_index * 2, 2, 0).astype(jnp.float32)
        delta_pair = lax.dynamic_slice_in_dim(delta_block, pair_index * 2, 2, 0).astype(jnp.float32)
        scores = (
            jnp.einsum("qhd,khd->hqk", queries, keys_pair, preferred_element_type=jnp.float32)
            * score_scale
        )
        probs = jnp.exp(scores - norm_pair[:, :, None])
        probs_b = probs.astype(jnp.bfloat16)
        grad_probs = jnp.einsum(
            "qhd,khd->hqk", grads_out, values_pair, preferred_element_type=jnp.float32
        )
        grad_scores = probs * (grad_probs - delta_pair[:, :, None])
        grad_scores_b = grad_scores.astype(jnp.bfloat16)
        value_part = jnp.einsum(
            "hqk,qhd->khd", probs_b, grads_out, preferred_element_type=jnp.float32
        )
        key_part = (
            jnp.einsum("hqk,qhd->khd", grad_scores_b, queries, preferred_element_type=jnp.float32)
            * score_scale
        )
        query_part = (
            jnp.einsum("hqk,khd->qhd", grad_scores_b, keys_pair, preferred_element_type=jnp.float32)
            * score_scale
        )
        grad_query = lax.dynamic_update_slice_in_dim(
            grad_query, query_part.reshape(query_rows, pair_width), column, 1
        )
        grad_key = lax.dynamic_update_slice_in_dim(
            grad_key, key_part.reshape(key_rows, pair_width), column, 1
        )
        grad_value = lax.dynamic_update_slice_in_dim(
            grad_value, value_part.reshape(key_rows, pair_width), column, 1
        )
        return (grad_query, grad_key, grad_value)

    start_totals = (
        jnp.zeros((query_rows, model_width), jnp.float32),
        jnp.zeros((key_rows, model_width), jnp.float32),
        jnp.zeros((key_rows, model_width), jnp.float32),
    )
    grad_query, grad_key, grad_value = lax.fori_loop(0, pair_count, head_pair, start_totals)
    query_owned = lax.psum_scatter(grad_query, "ka", scatter_dimension=0, tiled=True)
    dx_query = project(query_owned, weight_query).astype(jnp.bfloat16)
    combined = lax.psum_scatter(
        project(grad_key, weight_key) + project(grad_value, weight_value),
        "pb",
        scatter_dimension=0,
        tiled=True,
    )
    return (dx_query, combined.astype(jnp.bfloat16))


def solution(mesh):
    in_specs = (
        P(("pb", "ka"), None),
        P(("ka", "pb"), None),
        P(("ka", "pb"), None),
        P(("pb", "ka"), None),
        P(None, ("pb", "ka")),
        P(None, ("pb", "ka")),
        P(),
        P(),
        P(),
    )
    out_specs = (P(("pb", "ka"), None), P(("ka", "pb"), None))
    return jax.shard_map(local, mesh=mesh, in_specs=in_specs, out_specs=out_specs, check_vma=False)
```

profile of v0, /device:TPU:0, one launch (start us, length us, event | category | flops | bytes accessed | tf_op | source)
XLA Modules:
  0.0 247.1 jit_solution(18424641200395163584)
XLA Ops:
  8.7 6.4 %all-gather = bf16[4,32,16]{1,2,0:T(8,128)(2,1)S(1)} all-gather(bf16[1,32,16]{1,2,0:T(8,128)(2,1)} %bitcast.85), channel_id=1, replica_groups=mesh['pb'=8,'ka'=4] {'ka'}, dimensions={0}, use_global_device_ids=true | all-gather | bytes 5120 | tf_op jit(solution)/shard_map/all_gather | solution.py:31
  15.2 5.6 %all-gather.1 = bf16[4,32,16]{1,2,0:T(8,128)(2,1)S(1)} all-gather(bf16[1,32,16]{1,2,0:T(8,128)(2,1)} %bitcast.86), channel_id=1, replica_groups=mesh['pb'=8,'ka'=4] {'ka'}, dimensions={0}, use_global_device_ids=true | all-gather | bytes 5120 | tf_op jit(solution)/shard_map/all_gather | solution.py:32
  20.9 6.2 %all_gather.19 = bf16[128,1024]{1,0:T(8,128)(2,1)S(1)} all-gather(bf16[32,1024]{1,0:T(8,128)(2,1)} %param.11), channel_id=1, replica_groups=mesh['pb'=8,'ka'=4] {'ka'}, dimensions={0}, use_global_device_ids=true | all-gather | bytes 327680 | tf_op jit(solution)/shard_map/all_gather | solution.py:29
  27.0 7.8 %all_gather.21 = bf16[128,1024]{1,0:T(8,128)(2,1)} all-gather(bf16[32,1024]{1,0:T(8,128)(2,1)} %param.14), channel_id=1, replica_groups=mesh['pb'=8,'ka'=4] {'ka'}, dimensions={0}, use_global_device_ids=true | all-gather | bytes 327680 | tf_op jit(solution)/shard_map/all_gather | solution.py:30
  34.8 18.2 %all-gather.5.cloned.1.call-done = bf16[512,1024]{1,0:T(8,128)(2,1)} async-done(((bf16[64,1024]{1,0:T(8,128)(2,1)}), bf16[512,1024]{1,0:T(8,128)(2,1)}) %all-gather.5.cloned.1.call-update) | async-done | bytes 1048592 | tf_op jit(solution)/shard_map/all_gather | solution.py:35
  53.1 41.1 %all-gather.7.cloned.1.call-done = bf16[512,1024]{1,0:T(8,128)(2,1)} async-done(((bf16[64,1024]{1,0:T(8,128)(2,1)}), bf16[512,1024]{1,0:T(8,128)(2,1)}) %all-gather.7.cloned.1.call-update) | async-done | bytes 1048592 | tf_op jit(solution)/shard_map/all_gather | solution.py:36
  94.3 1.6 broadcast.30.clone
  95.9 1.6 broadcast.30
  97.5 42.1 %while.17 = (s32[]{:T(128)}, f32[128,1024]{1,0:T(8,128)S(1)}, f32[512,1024]{0,1:T(8,128)}, f32[512,1024]{0,1:T(8,128)}, bf16[512,1024]{1,0:T(8,128)(2,1)}, /*ind...) while((s32[]{:T(128)}, f32[128,1024]{1,0:T(8,128)S(1)}, ...), condition=%wide.region_1.0_spmd, body=%wide.region_0.0_spmd.sunk | while | flops 84754952 | bytes 6100249 | solution.py:97
  98.5 0.9 constant_dynamic-slice_fusion.13
  99.6 0.9 constant_dynamic-slice_fusion.10
  103.8 0.9 constant_dynamic-slice_fusion.13
  109.0 0.9 constant_dynamic-slice_fusion.13
  110.1 0.9 constant_dynamic-slice_fusion.10
  114.3 0.9 constant_dynamic-slice_fusion.13
  115.3 0.9 constant_dynamic-slice_fusion.10
  119.6 0.9 constant_dynamic-slice_fusion.13
  120.6 0.9 constant_dynamic-slice_fusion.10
  124.8 0.9 constant_dynamic-slice_fusion.13
  125.9 0.9 constant_dynamic-slice_fusion.10
  130.1 0.9 constant_dynamic-slice_fusion.13
  135.3 0.9 constant_dynamic-slice_fusion.13
  139.6 4.5 %fusion.14 = f32[512,1024]{1,0:T(8,128)} fusion(bf16[1024,1024]{1,0:T(8,128)(2,1)S(1)} %copy-done, f32[512,1024]{0,1:T(8,128)} %get-tuple-element.174), kind=kOutput, calls=%fused_computation.31 | convolution fusion | flops 1074266112 | bytes 6291456 | tf_op jit(solution)/shard_map/dot_general | solution.py:13
  144.0 2.6 %fusion.9 = f32[512,1024]{1,0:T(8,128)} fusion(bf16[1024,1024]{1,0:T(8,128)(2,1)S(1)} %copy-done, f32[512,1024]{0,1:T(8,128)S(1)} %copy-done.3), kind=kOutput, calls=%fused_computation.26 | convolution fusion | flops 1075838976 | bytes 6291456 | tf_op jit(solution)/shard_map/dot_general | solution.py:14
  146.8 3.7 %fusion.11 = f32[512,1024]{1,0:T(8,128)S(1)} fusion(bf16[1024,1024]{1,0:T(8,128)(2,1)} %param.19, f32[512,1024]{0,1:T(8,128)} %get-tuple-element.175), kind=kOutput, calls=%fused_computation.28 | convolution fusion | flops 1074266112 | bytes 6291456 | tf_op jit(solution)/shard_map/dot_general | solution.py:13
  151.6 2.7 %add_add_fusion = f32[512,1024]{1,0:T(8,128)} fusion(f32[512,1024]{1,0:T(8,128)S(1)} %fusion.11, f32[512,1024]{1,0:T(8,128)S(1)} %copy-done.6, f32[512,1024]{1,0:T(8,128)S(1)} %copy-done.7, bf16[1024,1024]{1,0:T(8,128)(2,1)S(1)} %copy-done.5, f32[512,1024]{0,1:T(8,128)S(1)} %copy-done.2), kind=kOutput, calls=%fused_computation.21 | convolution fusion | flops 1077411840 | bytes 12582912 | tf_op jit(solution)/shard_map/dot_general | solution.py:14
  154.3 13.0 %reduce-scatter.7.cloned.1.call-done = f32[32,1024]{1,0:T(8,128)} async-done(((f32[128,1024]{1,0:T(8,128)}), f32[32,1024]{1,0:T(8,128)}) %reduce-scatter.7.cloned.1.call-update) | async-done | bytes 131088
  167.2 1.1 copy.28
  168.3 2.5 fusion.17
  170.8 1.4 fusion.8
  172.2 66.7 %reduce-scatter.5.cloned.1.call-done = f32[64,1024]{1,0:T(8,128)} async-done(((f32[512,1024]{1,0:T(8,128)}), f32[64,1024]{1,0:T(8,128)}) %reduce-scatter.5.cloned.1.call-update) | async-done | bytes 262160 | tf_op jit(solution)/shard_map/reduce_scatter | solution.py:100
  238.9 1.6 convert_element_type.71
  (160 shorter events, 32.2 us)
Async XLA Ops:
  7.2 132.4 %copy-start = (bf16[1024,1024]{1,0:T(8,128)(2,1)S(1)}, bf16[1024,1024]{1,0:T(8,128)(2,1)}, u32[]{:S(2)}) copy-start(bf16[1024,1024]{1,0:T(8,128)(2,1)} %param.18) | copy-start | bytes 6291460
  7.2 45.9 %all-gather.5.cloned.1.call-start = ((), (), s32[]{:S(2)}) async-start(), calls=%async_computation.2 | async-start | bytes 1179648 | tf_op jit(solution)/shard_map/all_gather | solution.py:35
  7.9 86.3 %all-gather.7.cloned.1.call-start = ((), (), s32[]{:S(2)}) async-start(), calls=%async_computation.3 | async-start | bytes 1179648 | tf_op jit(solution)/shard_map/all_gather | solution.py:36
  8.7 158.6 %reduce-scatter.7.cloned.1.call-start = ((), (), s32[]{:S(2)}) async-start(), calls=%async_computation.5 | async-start | bytes 655360
  139.6 4.5 %copy-start.4 = (f32[128,1024]{1,0:T(8,128)}, f32[128,1024]{1,0:T(8,128)S(1)}, u32[]{:S(2)}) copy-start(f32[128,1024]{1,0:T(8,128)S(1)} %get-tuple-element.173) | copy-start | bytes 1572868
  139.6 4.5 %copy-start.3 = (f32[512,1024]{0,1:T(8,128)S(1)}, f32[512,1024]{0,1:T(8,128)}, u32[]{:S(2)}) copy-start(f32[512,1024]{0,1:T(8,128)} %get-tuple-element.174) | copy-start | bytes 6291460
  146.7 92.2 %reduce-scatter.5.cloned.1.call-start = ((), (), s32[]{:S(2)}) async-start(), calls=%async_computation.4 | async-start | bytes 2359296 | tf_op jit(solution)/shard_map/reduce_scatter | solution.py:100
  146.7 3.7 %copy-start.2 = (f32[512,1024]{0,1:T(8,128)S(1)}, f32[512,1024]{0,1:T(8,128)}, u32[]{:S(2)}) copy-start(f32[512,1024]{0,1:T(8,128)} %get-tuple-element.175) | copy-start | bytes 6291460
  146.8 3.7 %copy-start.5 = (bf16[1024,1024]{1,0:T(8,128)(2,1)S(1)}, bf16[1024,1024]{1,0:T(8,128)(2,1)}, u32[]{:S(2)}) copy-start(bf16[1024,1024]{1,0:T(8,128)(2,1)} %param.19) | copy-start | bytes 6291460
  146.8 4.1 %copy-start.6 = (f32[512,1024]{1,0:T(8,128)S(1)}, f32[512,1024]{1,0:T(8,128)}, u32[]{:S(2)}) copy-start(f32[512,1024]{1,0:T(8,128)} %fusion.14) | copy-start | bytes 6291460
  146.8 4.8 %copy-start.7 = (f32[512,1024]{1,0:T(8,128)S(1)}, f32[512,1024]{1,0:T(8,128)}, u32[]{:S(2)}) copy-start(f32[512,1024]{1,0:T(8,128)} %fusion.9) | copy-start | bytes 6291460
  168.3 2.5 %copy-start.1 = (bf16[1024,1024]{1,0:T(8,128)(2,1)S(1)}, bf16[1024,1024]{1,0:T(8,128)(2,1)}, u32[]{:S(2)}) copy-start(bf16[1024,1024]{1,0:T(8,128)(2,1)} %param.17) | copy-start | bytes 6291460
Sparse Core Ops, SparseCore 0:
  10.1 42.9 all-gather.4
  55.2 38.9 all-gather.6
  146.8 20.3 reduce-scatter.6
  170.6 68.2 reduce-scatter.4
where the time goes:
time: 248 us; the launch traced here: 247 us
  waiting for transfers between devices  140 us (56%)
  local copies, waits for them, and re-layouts  38.1 us (15%)
  matrix products  26.1 us (11%)
  blocking collectives  25.9 us (10%)
  between operations  13.9 us (6%)
    reduce_scatter x1, waiting for transfers between devices, local(): lax.psum_scatter(project(grad_key, weight_key) + project(grad_value, weig...  66.7 us
    all_gather x1, waiting for transfers between devices, local(): lax.all_gather(value_saved, 'pb', axis=0, tiled=True)  41.1 us
    dynamic_slice x64, local copies, waits for them, and re-layouts, columns(): lax.dynamic_slice_in_dim(source, column, pair_width, 1)  24.7 us
    all_gather x1, waiting for transfers between devices, local(): lax.all_gather(key_saved, 'pb', axis=0, tiled=True)  18.2 us
    unnamed x5, waiting for transfers between devices  14.4 us
    dot_general x3, matrix products, project(): lax.dot_general(upper, weights, contract, preferred_element_type=jnp.floa...  10.6 us
    all_gather x1, blocking collectives, local(): lax.all_gather(out_grad, 'ka', axis=0, tiled=True)  7.82 us
    dynamic_update_slice x8, local copies, waits for them, and re-layouts, head_pair(): lax.dynamic_update_slice_in_dim(grad_value, value_part.reshape(key_rows,...  6.93 us
  transfers between devices with their start and end apart: 4, of which 4 were waited for; matrix products, arithmetic and copies ran while one was open for 5% of the time, Pallas kernels for 0%

commit v1 on v0

v1 whole, which is shorter than its diff:
```python
import functools
import math

import jax
import jax.numpy as jnp
from jax import lax
from jax.experimental import pallas as pl
from jax.experimental.pallas import tpu as pltpu
from jax.sharding import PartitionSpec as P

HEAD_DIM = 64
LANES = 2 * HEAD_DIM
SCALE = 1.0 / HEAD_DIM**0.5
LOG2E = math.log2(math.e)
EXTRA = 8
TILE = 256
AXES = ("pb", "ka")
F32 = jnp.float32
BF16 = jnp.bfloat16
ROWS_BY_ROWS = (((1,), (1,)), ((), ()))


def low_lanes(rows):
    return lax.broadcasted_iota(jnp.int32, (rows, LANES), 1) < HEAD_DIM


def regroup(first, second):
    low = low_lanes(first.shape[0])
    mixed = pltpu.roll(jnp.where(low, second, first), HEAD_DIM, 1)
    return jnp.where(low, first, mixed), jnp.where(low, mixed, second)


def pack_kernel(n_ka, reps, sec, q_ref, k_ref, v_ref, g_ref, norm_ref, delta_ref, out_ref):
    heads, rows = norm_ref.shape
    kept = k_ref.shape[1]
    half = rows // 2
    me = lax.axis_index("pb") * n_ka + lax.axis_index("ka")
    slot = lax.rem(me, LANES // half)
    token = lax.broadcasted_iota(jnp.int32, (rows, 2 * LANES), 0)
    lane = lax.broadcasted_iota(jnp.int32, (rows, 2 * LANES), 1)
    target = slot * half + token + jnp.where(token < half, 0, LANES - half)
    place = jnp.where(lane == target, 1.0, 0.0).astype(BF16)
    both = jnp.concatenate([norm_ref[...], delta_ref[...]], axis=0)
    moved = jnp.dot(both, place, preferred_element_type=F32)
    stacked = jnp.concatenate(
        [
            moved[:heads, :LANES],
            moved[:heads, LANES:],
            moved[heads:, :LANES],
            moved[heads:, LANES:],
        ],
        axis=0,
    ).astype(BF16)
    row = lax.broadcasted_iota(jnp.int32, (heads * EXTRA, 4 * heads), 0)
    col = lax.broadcasted_iota(jnp.int32, (heads * EXTRA, 4 * heads), 1)
    kind = lax.rem(row, EXTRA)
    wanted = kind * heads + lax.div(row, EXTRA)
    pick = jnp.where((col == wanted) & (kind < 4), 1.0, 0.0).astype(BF16)
    extra = jnp.dot(pick, stacked, preferred_element_type=F32)

    for pair in range(heads // 2):
        cols = slice(pair * LANES, (pair + 1) * LANES)
        queries = regroup(q_ref[:, cols].astype(F32), g_ref[:, cols].astype(F32))
        keys = [
            regroup(k_ref[rep, :, cols].astype(F32), v_ref[rep, :, cols].astype(F32))
            for rep in range(reps)
        ]
        for side in range(2):
            head = 2 * pair + side
            query_rows = queries[side].astype(BF16)
            extra_rows = extra[head * EXTRA : (head + 1) * EXTRA].astype(BF16)
            for rep in range(reps):
                chunk = head * reps + rep
                out_ref[chunk, 0:rows, :] = query_rows
                if kept < sec:
                    out_ref[chunk, rows : rows + sec, :] = jnp.zeros((sec, LANES), BF16)
                out_ref[chunk, rows : rows + kept, :] = keys[rep][side].astype(BF16)
                out_ref[chunk, rows + sec : rows + sec + EXTRA, :] = extra_rows


def attend_kernel(rows, sec, in_ref, out_ref, kv_ref, kt_ref, acc_ref):
    count = in_ref.shape[0]
    half = rows // 2
    sources = TILE // half
    slots = LANES // half
    key_tiles = count * sec // TILE
    per_tile = TILE // sec
    low = low_lanes(TILE)

    for tile in range(key_tiles):
        part = in_ref[tile * per_tile : (tile + 1) * per_tile, rows : rows + sec, :]
        part = part.astype(F32).reshape(TILE, LANES)
        kv_ref[tile * TILE : (tile + 1) * TILE, :] = part.astype(BF16)
        kt_ref[:, tile * TILE : (tile + 1) * TILE] = part.T[:HEAD_DIM].astype(BF16)
    acc_ref[...] = jnp.zeros_like(acc_ref)

    def group(index):
        base = index * sources
        saved = jnp.concatenate(
            [
                in_ref[pl.ds(base + part * slots, slots), rows + sec : rows + sec + EXTRA, :]
                .astype(F32)
                .sum(0)
                for part in range(TILE // LANES)
            ],
            axis=1,
        )
        sides = []
        for side in range(2):
            block = in_ref[pl.ds(base, sources), side * half : (side + 1) * half, :]
            block = block.reshape(TILE, LANES).astype(F32)
            queries = jnp.where(low, block * SCALE, 0.0).astype(BF16)
            grads = jnp.where(low, 0.0, block).astype(BF16)
            norm = saved[side : side + 1] * LOG2E
            delta = saved[2 + side : 3 + side]
            grad_query = jnp.zeros((HEAD_DIM, TILE), F32)
            for tile in range(key_tiles):
                span = slice(tile * TILE, (tile + 1) * TILE)
                kv = kv_ref[span, :]
                scores = lax.dot_general(kv, queries, ROWS_BY_ROWS, preferred_element_type=F32)
                grad_probs = lax.dot_general(kv, grads, ROWS_BY_ROWS, preferred_element_type=F32)
                probs = jnp.exp2(scores * LOG2E - norm)
                grad_scores = (probs * (grad_probs - delta)).astype(BF16)
                probs = probs.astype(BF16)
                acc_ref[span, :] += jnp.dot(
                    grad_scores, queries, preferred_element_type=F32
                ) + jnp.dot(probs, grads, preferred_element_type=F32)
                grad_query += jnp.dot(kt_ref[:, span], grad_scores, preferred_element_type=F32)
            sides.append(grad_query)
        packed = (jnp.concatenate(sides, axis=0).T * SCALE).astype(BF16)
        out_ref[pl.ds(base, sources), sec : sec + half, :] = packed.reshape(sources, half, LANES)

    groups = count // sources
    if groups <= 2:
        for index in range(groups):
            group(index)
    else:
        lax.fori_loop(0, groups, lambda index, _: (group(index), 0)[1], 0)

    for tile in range(key_tiles):
        part = acc_ref[tile * TILE : (tile + 1) * TILE, :].reshape(per_tile, sec, LANES)
        out_ref[tile * per_tile : (tile + 1) * per_tile, 0:sec, :] = part.astype(BF16)


def project_kernel(
    reps, sec, in_ref, wq_ref, wk_ref, wv_ref, dxq_ref, dxkv_ref, gq_ref, gk_ref, gv_ref
):
    heads = in_ref.shape[0] // reps
    half = in_ref.shape[1] - sec
    for pair in range(heads // 2):
        cols = slice(pair * LANES, (pair + 1) * LANES)
        for rep in range(reps):
            even, odd = (
                in_ref[(2 * pair + side) * reps + rep, 0:sec, :].astype(F32) for side in range(2)
            )
            grad_key, grad_value = regroup(even, odd)
            span = slice(rep * sec, (rep + 1) * sec)
            gk_ref[span, cols] = grad_key.astype(BF16)
            gv_ref[span, cols] = grad_value.astype(BF16)
        even, odd = (
            in_ref[(2 * pair + side) * reps : (2 * pair + side + 1) * reps, sec : sec + half, :]
            .astype(F32)
            .sum(0)
            for side in range(2)
        )
        early, late = regroup(even, odd)
        gq_ref[0:half, cols] = early.astype(BF16)
        gq_ref[half : 2 * half, cols] = late.astype(BF16)

    def times(grads_ref, weight_ref):
        return lax.dot_general(
            grads_ref[...], weight_ref[...], ROWS_BY_ROWS, preferred_element_type=F32
        )

    dxq_ref[...] = times(gq_ref, wq_ref).astype(BF16)
    dxkv_ref[...] = (times(gk_ref, wk_ref) + times(gv_ref, wv_ref)).astype(BF16)


def vmem(count):
    return [pl.BlockSpec(memory_space=pltpu.VMEM)] * count


def local(
    n_ka,
    count,
    query_saved,
    key_saved,
    value_saved,
    out_grad,
    log_norm,
    row_delta,
    weight_query,
    weight_key,
    weight_value,
):
    rows, width = query_saved.shape
    key_rows = key_saved.shape[0]
    heads = width // HEAD_DIM
    reps = count // heads
    kept = key_rows // reps
    sec = -(-kept // 8) * 8
    half = rows // 2
    keys = count * sec

    sent = pl.pallas_call(
        functools.partial(pack_kernel, n_ka, reps, sec),
        out_shape=jax.ShapeDtypeStruct((count, rows + sec + EXTRA, LANES), BF16),
        in_specs=vmem(6),
        out_specs=pl.BlockSpec(memory_space=pltpu.VMEM),
    )(
        query_saved,
        key_saved.reshape(reps, kept, width),
        value_saved.reshape(reps, kept, width),
        out_grad,
        log_norm,
        row_delta,
    )
    held = lax.all_to_all(sent, AXES, 0, 0)
    grads = pl.pallas_call(
        functools.partial(attend_kernel, rows, sec),
        out_shape=jax.ShapeDtypeStruct((count, sec + half, LANES), BF16),
        in_specs=vmem(1),
        out_specs=pl.BlockSpec(memory_space=pltpu.VMEM),
        scratch_shapes=[
            pltpu.VMEM((keys, LANES), BF16),
            pltpu.VMEM((HEAD_DIM, keys), BF16),
            pltpu.VMEM((keys, LANES), F32),
        ],
    )(held)
    returned = lax.all_to_all(grads, AXES, 0, 0)
    dx_query, dx_keyvalue = pl.pallas_call(
        functools.partial(project_kernel, reps, sec),
        out_shape=(
            jax.ShapeDtypeStruct((rows, width), BF16),
            jax.ShapeDtypeStruct((reps * sec, width), BF16),
        ),
        in_specs=vmem(4),
        out_specs=tuple(vmem(2)),
        scratch_shapes=[
            pltpu.VMEM((rows, width), BF16),
            pltpu.VMEM((reps * sec, width), BF16),
            pltpu.VMEM((reps * sec, width), BF16),
        ],
    )(returned, weight_query, weight_key, weight_value)
    if kept != sec:
        dx_keyvalue = dx_keyvalue.reshape(reps, sec, width)[:, :kept].reshape(key_rows, width)
    return dx_query, dx_keyvalue


def solution(mesh):
    n_ka = mesh.shape["ka"]
    count = mesh.shape["pb"] * n_ka
    in_specs = (
        P(("pb", "ka"), None),
        P(("ka", "pb"), None),
        P(("ka", "pb"), None),
        P(("pb", "ka"), None),
        P(None, ("pb", "ka")),
        P(None, ("pb", "ka")),
        P(),
        P(),
        P(),
    )
    out_specs = (P(("pb", "ka"), None), P(("ka", "pb"), None))
    return jax.shard_map(
        functools.partial(local, n_ka, count),
        mesh=mesh,
        in_specs=in_specs,
        out_specs=out_specs,
        check_vma=False,
    )
```

time: 248 us -> 55.1 us (0.22)
  waiting for transfers between devices: 140 us -> 0 us
  local copies, waits for them, and re-layouts: 38.1 us -> 0 us
  matrix products: 26.1 us -> 0 us
  blocking collectives: 25.9 us -> 40.8 us
  Pallas kernels: 0 us -> 13.4 us
  between operations: 13.9 us -> 0.63 us
    reduce_scatter x1 -> x0, waiting for transfers between devices: 66.7 us -> none  [local(): lax.psum_scatter(project(grad_key, weight_key) + project(grad_value, weig...]
    all_gather x2 -> x0, waiting for transfers between devices: 59.4 us -> none  [the longest x1 41.1 us: local(): lax.all_gather(value_saved, 'pb', axis=0, tiled=True)]
    all_to_all x0 -> x2, blocking collectives: none -> 40.8 us  [the longest x1 24.2 us: local(): held = lax.all_to_all(sent, AXES, 0, 0)]
    dot_general x46 -> x0, matrix products: 26.1 us -> none  [the longest x3 10.6 us: project(): lax.dot_general(upper, weights, contract, preferred_element_type=jnp.floa...]
    all_gather x4 -> x0, blocking collectives: 25.9 us -> none  [the longest x1 7.82 us: local(): lax.all_gather(out_grad, 'ka', axis=0, tiled=True)]
    dynamic_slice x64 -> x0, local copies, waits for them, and re-layouts: 24.7 us -> none  [columns(): lax.dynamic_slice_in_dim(source, column, pair_width, 1)]
    unnamed x5 -> x0, waiting for transfers between devices: 14.4 us -> none
    pallas_call x0 -> x3, Pallas kernels: none -> 13.4 us  [the longest x1 5.69 us: local(): pl.pallas_call(functools.partial(project_kernel, reps, sec), out_shape=(j...]
  transfers between devices with their start and end apart: 4 -> 0, of which waited for: 4 -> 0; matrix products, arithmetic and copies ran while one was open for 5% -> 0% of each run, Pallas kernels for 0% -> 0%
where the time goes in v1:
time: 55.1 us; the launch traced here: 54.8 us
  blocking collectives  40.8 us (74%)
  Pallas kernels  13.4 us (24%)
  between operations  0.63 us (1%)
    all_to_all x1, blocking collectives, local(): held = lax.all_to_all(sent, AXES, 0, 0)  24.2 us
    all_to_all x1, blocking collectives, local(): returned = lax.all_to_all(grads, AXES, 0, 0)  16.6 us
    pallas_call x1, Pallas kernels, local(): pl.pallas_call(functools.partial(project_kernel, reps, sec), out_shape=(j...  5.69 us
    pallas_call x1, Pallas kernels, local(): pl.pallas_call(functools.partial(attend_kernel, rows, sec), out_shape=jax...  5.59 us
    pallas_call x1, Pallas kernels, local(): pl.pallas_call(functools.partial(pack_kernel, n_ka, reps, sec), out_shape...  2.11 us

profile of v1, /device:TPU:0, one launch (start us, length us, event | category | flops | bytes accessed | tf_op | source)
XLA Modules:
  0.0 54.8 jit_solution(9102705847284656430)
XLA Ops:
  0.6 2.1 %shard_map.104 = bf16[32,72,128]{2,1,0:T(8,128)(2,1)} custom-call(bf16[32,1024]{1,0:T(8,128)(2,1)} %q_ref.1, bf16[2,32,1024]{2,1,0:T(8,128)(2,1)} %bitcast.2, bf16[2,32,1024]{2,1,0:T(8,128)(2,1)} %bitcast.3, bf16[32,1024]{1,0:T(8,128)(2,1)} %g_ref.1, bf16[16,32]{1,0:T(8,128)(2,1)} %norm_ref.1, bf16[16,32]{1,0:T(8,128)(2,1)} %delta_ref.1), custom_call_target="tpu_custom_call" | custom-call | tf_op jit(solution)/shard_map/pallas_call | solution.py:205
  2.7 24.2 %all_to_all.10.in_ref = bf16[32,72,128]{2,1,0:T(8,128)(2,1)} all-to-all(bf16[32,72,128]{2,1,0:T(8,128)(2,1)} %shard_map.104), channel_id=1, replica_groups=mesh['pb'=8,'ka'=4] {'pb','ka'}, dimensions={0} | all-to-all | bytes 1179648 | tf_op jit(solution)/shard_map/all_to_all | solution.py:218
  27.0 5.6 %shard_map.105 = bf16[32,48,128]{2,1,0:T(8,128)(2,1)} custom-call(bf16[32,72,128]{2,1,0:T(8,128)(2,1)} %all_to_all.10.in_ref), custom_call_target="tpu_custom_call" | custom-call | tf_op jit(solution)/shard_map/pallas_call | solution.py:219
  32.6 16.6 %all_to_all.11.in_ref = bf16[32,48,128]{2,1,0:T(8,128)(2,1)} all-to-all(bf16[32,48,128]{2,1,0:T(8,128)(2,1)} %shard_map.105), channel_id=1, replica_groups=mesh['pb'=8,'ka'=4] {'pb','ka'}, dimensions={0} | all-to-all | bytes 786432 | tf_op jit(solution)/shard_map/all_to_all | solution.py:230
  49.1 5.7 %shard_map.106 = (bf16[32,1024]{1,0:T(8,128)(2,1)}, bf16[64,1024]{1,0:T(8,128)(2,1)}) custom-call(bf16[32,48,128]{2,1,0:T(8,128)(2,1)} %all_to_all.11.in_ref, bf16[1024,1024]{1,0:T(8,128)(2,1)} %wq_ref.1, bf16[1024,1024]{1,0:T(8,128)(2,1)} %wk_ref.1, bf16[1024,1024]{1,0:T(8,128)(2,1)} %wv_ref.1), custom_call_target="tpu_custom_call" | custom-call | tf_op jit(solution)/shard_map/pallas_call | solution.py:231

commit v2 on v1

--- a/solution.py
+++ b/solution.py
@@ -12,6 +12,7 @@
 LANES = 2 * HEAD_DIM
 SCALE = 1.0 / HEAD_DIM**0.5
 LOG2E = math.log2(math.e)
+PARAMS = pltpu.CompilerParams(vmem_limit_bytes=24 * 1024 * 1024)
 EXTRA = 8
 TILE = 256
 AXES = ("pb", "ka")
@@ -30,7 +31,17 @@
     return jnp.where(low, first, mixed), jnp.where(low, mixed, second)
 
 
-def pack_kernel(n_ka, reps, sec, q_ref, k_ref, v_ref, g_ref, norm_ref, delta_ref, out_ref):
+def pack_kernel(n_ka, reps, sec, *refs):
+    sources, out_ref, (*held, sems) = refs[:6], refs[6], refs[7:]
+    copies = [
+        pltpu.make_async_copy(source, target, sems.at[index])
+        for index, (source, target) in enumerate(zip(sources, held))
+    ]
+    for copy in copies:
+        copy.start()
+    for copy in copies:
+        copy.wait()
+    q_ref, g_ref, k_ref, v_ref, norm_ref, delta_ref = held
     heads, rows = norm_ref.shape
     kept = k_ref.shape[1]
     half = rows // 2
@@ -78,7 +89,14 @@
                 out_ref[chunk, rows + sec : rows + sec + EXTRA, :] = extra_rows
 
 
-def attend_kernel(rows, sec, in_ref, out_ref, kv_ref, kt_ref, acc_ref):
+def attend_kernel(rows, sec, in_ref, *refs):
+    weights, out_ref, near, (kv_ref, kt_ref, acc_ref, sems) = refs[:3], refs[3], refs[4:7], refs[7:]
+    copies = [
+        pltpu.make_async_copy(source, target, sems.at[index])
+        for index, (source, target) in enumerate(zip(weights, near))
+    ]
+    for copy in copies:
+        copy.start()
     count = in_ref.shape[0]
     half = rows // 2
     sources = TILE // half
@@ -140,6 +158,8 @@
     for tile in range(key_tiles):
         part = acc_ref[tile * TILE : (tile + 1) * TILE, :].reshape(per_tile, sec, LANES)
         out_ref[tile * per_tile : (tile + 1) * per_tile, 0:sec, :] = part.astype(BF16)
+    for copy in copies:
+        copy.wait()
 
 
 def project_kernel(
@@ -176,8 +196,12 @@
     dxkv_ref[...] = (times(gk_ref, wk_ref) + times(gv_ref, wv_ref)).astype(BF16)
 
 
-def vmem(count):
+def in_vmem(count):
     return [pl.BlockSpec(memory_space=pltpu.VMEM)] * count
+
+
+def in_hbm(count):
+    return [pl.BlockSpec(memory_space=pltpu.HBM)] * count
 
 
 def local(
@@ -202,31 +226,39 @@
     half = rows // 2
     keys = count * sec
 
+    inputs = [
+        query_saved,
+        out_grad,
+        key_saved.reshape(reps, kept, width),
+        value_saved.reshape(reps, kept, width),
+        log_norm,
+        row_delta,
+    ]
     sent = pl.pallas_call(
         functools.partial(pack_kernel, n_ka, reps, sec),
-        out_shape=jax.ShapeDtypeStruct((count, rows + sec + EXTRA, LANES), BF16),
-        in_specs=vmem(6),
-        out_specs=pl.BlockSpec(memory_space=pltpu.VMEM),
-    )(
-        query_saved,
-        key_saved.reshape(reps, kept, width),
-        value_saved.reshape(reps, kept, width),
-        out_grad,
-        log_norm,
-        row_delta,
-    )
+        out_shape=pltpu.VMEM((count, rows + sec + EXTRA, LANES), BF16),
+        in_specs=in_hbm(6),
+        out_specs=in_vmem(1)[0],
+        scratch_shapes=[pltpu.VMEM(array.shape, BF16) for array in inputs]
+        + [pltpu.SemaphoreType.DMA((6,))],
+        compiler_params=PARAMS,
+    )(*[pltpu.with_memory_space_constraint(array, pltpu.HBM) for array in inputs])
     held = lax.all_to_all(sent, AXES, 0, 0)
-    grads = pl.pallas_call(
+    weights = [weight_query, weight_key, weight_value]
+    grads, *weights = pl.pallas_call(
         functools.partial(attend_kernel, rows, sec),
-        out_shape=jax.ShapeDtypeStruct((count, sec + half, LANES), BF16),
-        in_specs=vmem(1),
-        out_specs=pl.BlockSpec(memory_space=pltpu.VMEM),
+        out_shape=[pltpu.VMEM((count, sec + half, LANES), BF16)]
+        + [pltpu.VMEM(weight.shape, BF16) for weight in weights],
+        in_specs=in_vmem(1) + in_hbm(3),
+        out_specs=in_vmem(4),
         scratch_shapes=[
             pltpu.VMEM((keys, LANES), BF16),
             pltpu.VMEM((HEAD_DIM, keys), BF16),
             pltpu.VMEM((keys, LANES), F32),
+            pltpu.SemaphoreType.DMA((3,)),
         ],
-    )(held)
+        compiler_params=PARAMS,
+    )(held, *[pltpu.with_memory_space_constraint(weight, pltpu.HBM) for weight in weights])
     returned = lax.all_to_all(grads, AXES, 0, 0)
     dx_query, dx_keyvalue = pl.pallas_call(
         functools.partial(project_kernel, reps, sec),
@@ -234,14 +266,15 @@
             jax.ShapeDtypeStruct((rows, width), BF16),
             jax.ShapeDtypeStruct((reps * sec, width), BF16),
         ),
-        in_specs=vmem(4),
-        out_specs=tuple(vmem(2)),
+        in_specs=in_vmem(4),
+        out_specs=tuple(in_vmem(2)),
         scratch_shapes=[
             pltpu.VMEM((rows, width), BF16),
             pltpu.VMEM((reps * sec, width), BF16),
             pltpu.VMEM((reps * sec, width), BF16),
         ],
-    )(returned, weight_query, weight_key, weight_value)
+        compiler_params=PARAMS,
+    )(returned, *weights)
     if kept != sec:
         dx_keyvalue = dx_keyvalue.reshape(reps, sec, width)[:, :kept].reshape(key_rows, width)
     return dx_query, dx_keyvalue

time: 55.1 us -> 48.9 us (0.89)
  Pallas kernels: 13.4 us -> 7.88 us
  blocking collectives: 40.8 us -> 40.2 us
    pallas_call x1, Pallas kernels: 5.69 us -> 2.7 us  [local(): pl.pallas_call(functools.partial(project_kernel, reps, sec), out_shape=(j...]
    pallas_call x1, Pallas kernels: 5.59 us -> 3.83 us  [local(): pl.pallas_call(functools.partial(attend_kernel, rows, sec), out_shape=[pl...]
    pallas_call x1, Pallas kernels: 2.11 us -> 1.36 us  [local(): pl.pallas_call(functools.partial(pack_kernel, n_ka, reps, sec), out_shape...]
where the time goes in v2:
time: 48.9 us; the launch traced here: 48.7 us
  blocking collectives  40.2 us (82%)
  Pallas kernels  7.88 us (16%)
  between operations  0.65 us (1%)
    all_to_all x1, blocking collectives, local(): held = lax.all_to_all(sent, AXES, 0, 0)  23.9 us
    all_to_all x1, blocking collectives, local(): returned = lax.all_to_all(grads, AXES, 0, 0)  16.2 us
    pallas_call x1, Pallas kernels, local(): pl.pallas_call(functools.partial(attend_kernel, rows, sec), out_shape=[pl...  3.83 us
    pallas_call x1, Pallas kernels, local(): pl.pallas_call(functools.partial(project_kernel, reps, sec), out_shape=(j...  2.7 us
    pallas_call x1, Pallas kernels, local(): pl.pallas_call(functools.partial(pack_kernel, n_ka, reps, sec), out_shape...  1.36 us

profile of v2, /device:TPU:0, one launch (start us, length us, event | category | flops | bytes accessed | tf_op | source)
XLA Modules:
  0.0 48.7 jit_solution(893844157682453901)
XLA Ops:
  0.6 1.4 %shard_map.104 = bf16[32,72,128]{2,1,0:T(8,128)(2,1)S(1)} custom-call(bf16[32,1024]{1,0:T(8,128)(2,1)} %refs_0_.2, bf16[32,1024]{1,0:T(8,128)(2,1)} %refs_1_.2, bf16[2,32,1024]{2,1,0:T(8,128)(2,1)} %bitcast.2, bf16[2,32,1024]{2,1,0:T(8,128)(2,1)} %bitcast.3, bf16[16,32]{1,0:T(8,128)(2,1)} %refs_4_.1, bf16[16,32]{1,0:T(8,128)(2,1)} %refs_5_.1), custom_call_target="tpu_custom_call" | custom-call | tf_op jit(solution)/shard_map/pallas_call | solution.py:237
  2.0 23.9 %all_to_all.10.in_ref = bf16[32,72,128]{2,1,0:T(8,128)(2,1)S(1)} all-to-all(bf16[32,72,128]{2,1,0:T(8,128)(2,1)S(1)} %shard_map.104), channel_id=1, replica_groups=mesh['pb'=8,'ka'=4] {'pb','ka'}, dimensions={0} | all-to-all | bytes 1179648 | tf_op jit(solution)/shard_map/all_to_all | solution.py:246
  25.9 3.8 %shard_map.105 = (bf16[32,48,128]{2,1,0:T(8,128)(2,1)S(1)}, bf16[1024,1024]{1,0:T(8,128)(2,1)S(1)}, bf16[1024,1024]{1,0:T(8,128)(2,1)S(1)}, bf16[1024,1024]{1,0:T(8,128)(2,1)S(1)}) custom-call(bf16[32,72,128]{2,1,0:T(8,128)(2,1)S(1)} %all_to_all.10.in_ref, bf16[1024,1024]{1,0:T(8,128)(2,1)} %refs_0_.3, bf16[1024,1024]{1,0:T(8,128)(2,1)} %refs_1_.3, ...), custom_call_target="tpu_custom_call" | custom-call | tf_op jit(solution)/shard_map/pallas_call | solution.py:248
  29.8 16.2 %all_to_all.11.in_ref = bf16[32,48,128]{2,1,0:T(8,128)(2,1)S(1)} all-to-all(bf16[32,48,128]{2,1,0:T(8,128)(2,1)S(1)} %get-tuple-element.6), channel_id=1, replica_groups=mesh['pb'=8,'ka'=4] {'pb','ka'}, dimensions={0} | all-to-all | bytes 786432 | tf_op jit(solution)/shard_map/all_to_all | solution.py:262
  46.0 2.7 %shard_map.106 = (bf16[32,1024]{1,0:T(8,128)(2,1)}, bf16[64,1024]{1,0:T(8,128)(2,1)}) custom-call(bf16[32,48,128]{2,1,0:T(8,128)(2,1)S(1)} %all_to_all.11.in_ref, bf16[1024,1024]{1,0:T(8,128)(2,1)S(1)} %get-tuple-element.7.wq_ref, bf16[1024,1024]{1,0:T(8,128)(2,1)S(1)} %get-tuple-element.8.wk_ref, bf16[1024,1024]{1,0:T(8,128)(2,1)S(1)} %get-tuple-element.9.wv_ref), custom_call_target="tpu_custom_call" | custom-call | tf_op jit(solution)/shard_map/pallas_call | solution.py:263

commit v3 on v2

v3 whole, which is shorter than its diff:
```python
import functools
import math

import jax
import jax.numpy as jnp
from jax import lax
from jax.experimental import pallas as pl
from jax.experimental.pallas import tpu as pltpu
from jax.sharding import PartitionSpec as P

HEAD_DIM = 64
LANES = 2 * HEAD_DIM
SCALE = 1.0 / HEAD_DIM**0.5
LOG2E = math.log2(math.e)
TILE = 256
VMEM_LIMIT = 24 * 1024 * 1024
PARAMS = pltpu.CompilerParams(vmem_limit_bytes=VMEM_LIMIT)
AXES = ("pb", "ka")
F32 = jnp.float32
BF16 = jnp.bfloat16
ROWS_BY_ROWS = (((1,), (1,)), ((), ()))


def low_lanes(rows):
    return lax.broadcasted_iota(jnp.int32, (rows, LANES), 1) < HEAD_DIM


def regroup(first, second):
    low = low_lanes(first.shape[0])
    mixed = pltpu.roll(jnp.where(low, second, first), HEAD_DIM, 1)
    return jnp.where(low, first, mixed), jnp.where(low, mixed, second)


def fetch(sources, targets, sems):
    copies = [
        pltpu.make_async_copy(source, target, sems.at[index])
        for index, (source, target) in enumerate(zip(sources, targets))
    ]
    for copy in copies:
        copy.start()
    return copies


def pack_kernel(n_ka, reps, sec, *refs):
    sources, out_ref, (*held, sems) = refs[:6], refs[6], refs[7:]
    for copy in fetch(sources, held, sems):
        copy.wait()
    q_ref, g_ref, k_ref, v_ref, norm_ref, delta_ref = held
    heads, rows = norm_ref.shape
    kept = k_ref.shape[1]
    half = rows // 2
    size = sec + half + 2
    me = lax.axis_index("pb") * n_ka + lax.axis_index("ka")
    slot = lax.rem(me, LANES // half)
    token = lax.broadcasted_iota(jnp.int32, (rows, 2 * LANES), 0)
    lane = lax.broadcasted_iota(jnp.int32, (rows, 2 * LANES), 1)
    quarter = half // 2
    target = (
        lax.div(token, half) * LANES
        + lax.rem(lax.div(token, quarter), 2) * HEAD_DIM
        + slot * quarter
        + lax.rem(token, quarter)
    )
    place = jnp.where(lane == target, 1.0, 0.0).astype(BF16)
    both = jnp.concatenate([norm_ref[...], delta_ref[...]], axis=0)
    moved = jnp.dot(both, place, preferred_element_type=F32)
    stacked = jnp.concatenate(
        [
            moved[:heads, :LANES],
            moved[:heads, LANES:],
            moved[heads:, :LANES],
            moved[heads:, LANES:],
        ],
        axis=0,
    ).astype(BF16)
    row = lax.broadcasted_iota(jnp.int32, (heads * 4, heads * 4), 0)
    col = lax.broadcasted_iota(jnp.int32, (heads * 4, heads * 4), 1)
    inner = lax.rem(row, 4)
    wanted = (lax.rem(inner, 2) * 2 + lax.div(inner, 2)) * heads + lax.div(row, 4)
    pick = jnp.where(col == wanted, 1.0, 0.0).astype(BF16)
    extra = jnp.dot(pick, stacked, preferred_element_type=F32)

    for pair in range(heads // 2):
        cols = slice(pair * LANES, (pair + 1) * LANES)
        queries = regroup(q_ref[:, cols].astype(F32), g_ref[:, cols].astype(F32))
        keys = [
            regroup(k_ref[rep, :, cols].astype(F32), v_ref[rep, :, cols].astype(F32))
            for rep in range(reps)
        ]
        for which in range(2):
            head = 2 * pair + which
            for rep in range(reps):
                base = (head * reps + rep) * size
                side = rep % 2
                key_rows = keys[rep][which]
                if kept < sec:
                    key_rows = jnp.concatenate([key_rows, jnp.zeros((sec - kept, LANES), F32)], axis=0)
                out_ref[base : base + sec, :] = key_rows.astype(BF16)
                out_ref[base + sec : base + sec + half, :] = queries[which][
                    side * half : (side + 1) * half
                ].astype(BF16)
                first = head * 4 + side * 2
                out_ref[base + sec + half : base + size, :] = extra[first : first + 2].astype(BF16)


def split_kernel(count, sec, half, in_ref, own_ref):
    size = sec + half + 2
    quarter = half // 2
    slots = LANES // half
    saved = []
    for group in range(count // slots):
        total = None
        for source in range(group * slots, (group + 1) * slots):
            base = source * size + sec
            for part in range(2):
                row = (part * count + source) * quarter
                own_ref[row : row + quarter, :] = in_ref[
                    base + part * quarter : base + (part + 1) * quarter, :
                ]
            extra = in_ref[base + half : base + half + 2, :].astype(F32)
            total = extra if total is None else total + extra
        saved.append(total)
    pairs = [regroup(saved[group], saved[group + 1]) for group in range(0, len(saved), 2)]
    rows = [pair[part][kind : kind + 1] for kind in range(2) for part in range(2) for pair in pairs]
    base = count * half
    own_ref[base : base + len(rows), :] = jnp.concatenate(rows, axis=0).astype(BF16)


def attend(queries_ref, saved_ref, kv_ref, kt_ref, gq_ref, emit):
    keys = kv_ref.shape[0]
    low = low_lanes(TILE)
    blocks = gq_ref.shape[0]
    rows = TILE // LANES
    saved_ref[...] = queries_ref[blocks * TILE :, :].astype(F32)

    def step(pair):
        sides = []
        for index in (2 * pair, 2 * pair + 1):
            start = index * TILE
            if not isinstance(start, int):
                start = pl.multiple_of(start, TILE)
            block = queries_ref[pl.ds(start, TILE), :].astype(F32)
            queries = jnp.where(low, block * SCALE, 0.0).astype(BF16)
            grads = jnp.where(low, 0.0, block).astype(BF16)
            norm, delta = (
                jnp.concatenate(
                    [
                        saved_ref[pl.ds((kind * blocks + index) * rows + row, 1), :]
                        for row in range(rows)
                    ],
                    axis=1,
                )
                for kind in range(2)
            )
            sides.append((queries, grads, norm * LOG2E, delta))
        totals = [None, None]
        for tile in range(keys // TILE):
            span = slice(tile * TILE, (tile + 1) * TILE)
            kv = kv_ref[span, :]
            part = None
            for side, (queries, grads, norm, delta) in enumerate(sides):
                scores = lax.dot_general(kv, queries, ROWS_BY_ROWS, preferred_element_type=F32)
                grad_probs = lax.dot_general(kv, grads, ROWS_BY_ROWS, preferred_element_type=F32)
                probs = jnp.exp2(scores * LOG2E - norm)
                grad_scores = (probs * (grad_probs - delta)).astype(BF16)
                first = jnp.dot(probs.astype(BF16), grads, preferred_element_type=F32)
                part = first if part is None else part + first
                part += jnp.dot(grad_scores, queries, preferred_element_type=F32)
                more = jnp.dot(kt_ref[:, span], grad_scores, preferred_element_type=F32)
                totals[side] = more if totals[side] is None else totals[side] + more
            emit(span, part)
        for side in range(2):
            gq_ref[2 * pair + side] = totals[side]

    if blocks == 2:
        step(0)
    else:
        lax.fori_loop(0, blocks // 2, lambda pair, _: (step(pair), 0)[1], 0)


def own_kernel(count, sec, half, in_ref, queries_ref, *refs):
    weights, (kv_ref, kt_ref, acc_ref, gqb_ref), near, (gq_ref, saved_ref, sems) = (
        refs[:2],
        refs[2:6],
        refs[6:8],
        refs[8:],
    )
    copies = fetch(weights, near, sems)
    size = sec + half + 2
    per_tile = TILE // sec
    for tile in range(count * sec // TILE):
        span = slice(tile * TILE, (tile + 1) * TILE)
        part = jnp.concatenate(
            [
                in_ref[source * size : source * size + sec, :].astype(F32)
                for source in range(tile * per_tile, (tile + 1) * per_tile)
            ],
            axis=0,
        )
        kv_ref[span, :] = part.astype(BF16)
        kt_ref[:, span] = part.T[:HEAD_DIM].astype(BF16)

    once = gq_ref.shape[0] == 2
    if not once:
        acc_ref[...] = jnp.zeros_like(acc_ref)

    def emit(span, part):
        acc_ref[span, :] = part if once else acc_ref[span, :] + part

    attend(queries_ref, saved_ref, kv_ref, kt_ref, gq_ref, emit)
    gqb_ref[...] = gq_ref[...].astype(BF16)
    for copy in copies:
        copy.wait()


def far_kernel(queries_ref, kv_ref, kt_ref, start_ref, weight_ref, *refs):
    dkv_ref, gq_ref, near_ref, acc_ref, saved_ref, sems = refs
    copies = fetch([weight_ref], [near_ref], sems)
    once = gq_ref.shape[0] == 2
    if not once:
        acc_ref[...] = start_ref[...]

    def emit(span, part):
        if once:
            dkv_ref[span, :] = (start_ref[span, :] + part).astype(BF16)
        else:
            acc_ref[span, :] += part

    attend(queries_ref, saved_ref, kv_ref, kt_ref, gq_ref, emit)
    if not once:
        dkv_ref[...] = acc_ref[...].astype(BF16)
    for copy in copies:
        copy.wait()


def gather_kernel(count, sec, quarter, dkv_ref, gq_ref, other_ref, out_ref):
    size = sec + quarter
    blocks = gq_ref.shape[0]
    for source in range(count):
        out_ref[source * size : source * size + sec, :] = dkv_ref[source * sec : (source + 1) * sec, :]
    for index in range(blocks // 2):
        both = jnp.concatenate(
            [
                gq_ref[block] + other_ref[block].astype(F32)
                for block in (index, index + blocks // 2)
            ],
            axis=0,
        )
        packed = both.T * SCALE
        for offset in range(TILE // quarter):
            base = (index * (TILE // quarter) + offset) * size + sec
            out_ref[base : base + quarter, :] = packed[
                offset * quarter : (offset + 1) * quarter
            ].astype(BF16)


def project_kernel(
    reps, sec, quarter, in_ref, wq_ref, wk_ref, wv_ref, dxq_ref, dxkv_ref, gq_ref, gk_ref, gv_ref
):
    size = sec + quarter
    heads = in_ref.shape[0] // (reps * size)
    for pair in range(heads // 2):
        cols = slice(pair * LANES, (pair + 1) * LANES)
        totals = [[None, None], [None, None]]
        for rep in range(reps):
            bases = [((2 * pair + which) * reps + rep) * size for which in range(2)]
            even, odd = (in_ref[base : base + sec, :].astype(F32) for base in bases)
            grad_key, grad_value = regroup(even, odd)
            span = slice(rep * sec, (rep + 1) * sec)
            gk_ref[span, cols] = grad_key.astype(BF16)
            gv_ref[span, cols] = grad_value.astype(BF16)
            side = 1 - rep % 2
            for which, base in enumerate(bases):
                part = in_ref[base + sec : base + size, :].astype(F32)
                before = totals[side][which]
                totals[side][which] = part if before is None else before + part
        for side in range(2):
            for part, rows in enumerate(regroup(*totals[side])):
                first = (2 * side + part) * quarter
                gq_ref[first : first + quarter, cols] = rows.astype(BF16)

    def times(grads_ref, weight_ref):
        return lax.dot_general(
            grads_ref[...], weight_ref[...], ROWS_BY_ROWS, preferred_element_type=F32
        )

    dxq_ref[...] = times(gq_ref, wq_ref).astype(BF16)
    dxkv_ref[...] = (times(gk_ref, wk_ref) + times(gv_ref, wv_ref)).astype(BF16)


def in_vmem(count):
    return [pl.BlockSpec(memory_space=pltpu.VMEM)] * count


def in_hbm(count):
    return [pl.BlockSpec(memory_space=pltpu.HBM)] * count


def keep_in_hbm(arrays):
    return [pltpu.with_memory_space_constraint(array, pltpu.HBM) for array in arrays]


def exchange(packed, count):
    chunks = packed.reshape(count, packed.shape[0] // (2 * count), 2, LANES)
    return lax.all_to_all(chunks, AXES, 0, 0).reshape(packed.shape)


def local(
    n_ka,
    count,
    query_saved,
    key_saved,
    value_saved,
    out_grad,
    log_norm,
    row_delta,
    weight_query,
    weight_key,
    weight_value,
):
    rows, width = query_saved.shape
    key_rows = key_saved.shape[0]
    heads = width // HEAD_DIM
    reps = count // heads
    kept = key_rows // reps
    sec = -(-kept // 8) * 8
    half = rows // 2
    keys = count * sec
    queries = count * half
    if reps % 2 or queries % (2 * TILE) or keys % TILE:
        raise ValueError("sizes")

    inputs = [
        query_saved,
        out_grad,
        key_saved.reshape(reps, kept, width),
        value_saved.reshape(reps, kept, width),
        log_norm,
        row_delta,
    ]
    sent = pl.pallas_call(
        functools.partial(pack_kernel, n_ka, reps, sec),
        out_shape=pltpu.VMEM((count * (sec + half + 2), LANES), BF16),
        in_specs=in_hbm(6),
        out_specs=in_vmem(1)[0],
        scratch_shapes=[pltpu.VMEM(array.shape, BF16) for array in inputs]
        + [pltpu.SemaphoreType.DMA((6,))],
        compiler_params=PARAMS,
    )(*keep_in_hbm(inputs))
    held = exchange(sent, count)
    own = pl.pallas_call(
        functools.partial(split_kernel, count, sec, half),
        out_shape=pltpu.VMEM((queries + queries * 2 // LANES, LANES), BF16),
        in_specs=in_vmem(1),
        out_specs=in_vmem(1)[0],
        compiler_params=PARAMS,
    )(held)
    twins = [(index, index ^ 1) for index in range(count)]
    far = lax.ppermute(own, AXES, twins)
    work = pl.CostEstimate(
        flops=10 * queries * keys * HEAD_DIM, transcendentals=queries * keys, bytes_accessed=1 << 20
    )
    blocks = queries // TILE
    saved = pltpu.VMEM((2 * queries // LANES, LANES), F32)
    kv, kt, acc, own_part, near_key, near_value = pl.pallas_call(
        functools.partial(own_kernel, count, sec, half),
        out_shape=[
            pltpu.VMEM((keys, LANES), BF16),
            pltpu.VMEM((HEAD_DIM, keys), BF16),
            pltpu.VMEM((keys, LANES), F32),
            pltpu.VMEM((blocks, HEAD_DIM, TILE), BF16),
            pltpu.VMEM(weight_key.shape, BF16),
            pltpu.VMEM(weight_value.shape, BF16),
        ],
        in_specs=in_vmem(2) + in_hbm(2),
        out_specs=in_vmem(6),
        scratch_shapes=[
            pltpu.VMEM((blocks, HEAD_DIM, TILE), F32),
            saved,
            pltpu.SemaphoreType.DMA((2,)),
        ],
        compiler_params=PARAMS,
        cost_estimate=work,
    )(held, own, *keep_in_hbm([weight_key, weight_value]))
    other_part = lax.ppermute(own_part, AXES, twins)
    grad_keyvalue, far_part, near_query = pl.pallas_call(
        far_kernel,
        out_shape=[
            pltpu.VMEM((keys, LANES), BF16),
            pltpu.VMEM((blocks, HEAD_DIM, TILE), F32),
            pltpu.VMEM(weight_query.shape, BF16),
        ],
        in_specs=in_vmem(4) + in_hbm(1),
        out_specs=in_vmem(3),
        scratch_shapes=[pltpu.VMEM((keys, LANES), F32), saved, pltpu.SemaphoreType.DMA((1,))],
        compiler_params=PARAMS,
        cost_estimate=work,
    )(far, kv, kt, acc, *keep_in_hbm([weight_query]))
    grads = pl.pallas_call(
        functools.partial(gather_kernel, count, sec, half // 2),
        out_shape=pltpu.VMEM((count * (sec + half // 2), LANES), BF16),
        in_specs=in_vmem(3),
        out_specs=in_vmem(1)[0],
        compiler_params=PARAMS,
    )(grad_keyvalue, far_part, other_part)
    returned = exchange(grads, count)
    dx_query, dx_keyvalue = pl.pallas_call(
        functools.partial(project_kernel, reps, sec, half // 2),
        out_shape=(
            jax.ShapeDtypeStruct((rows, width), BF16),
            jax.ShapeDtypeStruct((reps * sec, width), BF16),
        ),
        in_specs=in_vmem(4),
        out_specs=tuple(in_vmem(2)),
        scratch_shapes=[
            pltpu.VMEM((rows, width), BF16),
            pltpu.VMEM((reps * sec, width), BF16),
            pltpu.VMEM((reps * sec, width), BF16),
        ],
        compiler_params=PARAMS,
    )(returned, near_query, near_key, near_value)
    if kept != sec:
        dx_keyvalue = dx_keyvalue.reshape(reps, sec, width)[:, :kept].reshape(key_rows, width)
    return dx_query, dx_keyvalue


def solution(mesh):
    n_ka = mesh.shape["ka"]
    count = mesh.shape["pb"] * n_ka
    in_specs = (
        P(("pb", "ka"), None),
        P(("ka", "pb"), None),
        P(("ka", "pb"), None),
        P(("pb", "ka"), None),
        P(None, ("pb", "ka")),
        P(None, ("pb", "ka")),
        P(),
        P(),
        P(),
    )
    out_specs = (P(("pb", "ka"), None), P(("ka", "pb"), None))
    return jax.shard_map(
        functools.partial(local, n_ka, count),
        mesh=mesh,
        in_specs=in_specs,
        out_specs=out_specs,
        check_vma=False,
    )
```

time: 48.9 us -> 45.1 us (0.922)
  blocking collectives: 40.2 us -> 35.1 us
  Pallas kernels: 7.88 us -> 8.56 us
  starting transfers between devices: 0 us -> 0.6 us
    all_to_all x2, blocking collectives: 40.2 us -> 35.1 us  [exchange(): return lax.all_to_all(chunks, AXES, 0, 0).reshape(packed.shape)]
    pallas_call x2 -> x5, Pallas kernels: 6.52 us -> 7.2 us  [the longest x1 2.69 us: local(): pl.pallas_call(functools.partial(project_kernel, reps, sec, half // 2), o...]
    ppermute x0 -> x2, starting transfers between devices: none -> 0.6 us  [the longest x1 0.56 us: local(): other_part = lax.ppermute(own_part, AXES, twins)]
  transfers between devices with their start and end apart: 0 -> 2, of which waited for: 0 -> 0; matrix products, arithmetic and copies ran while one was open for 0% -> 0% of each run, Pallas kernels for 0% -> 10%
where the time goes in v3:
time: 45.1 us; the launch traced here: 45 us
  blocking collectives  35.1 us (78%)
  Pallas kernels  8.56 us (19%)
  between operations  0.68 us (2%)
  starting transfers between devices  0.6 us (1%)
    all_to_all x2, blocking collectives, exchange(): return lax.all_to_all(chunks, AXES, 0, 0).reshape(packed.shape)  35.1 us
    pallas_call x1, Pallas kernels, local(): pl.pallas_call(functools.partial(project_kernel, reps, sec, half // 2), o...  2.69 us
    pallas_call x1, Pallas kernels, local(): pl.pallas_call(functools.partial(own_kernel, count, sec, half), out_shape...  2.24 us
    pallas_call x1, Pallas kernels, local(): pl.pallas_call(far_kernel, out_shape=[pltpu.VMEM((keys, LANES), BF16), pl...  2.07 us
    pallas_call x1, Pallas kernels, local(): pl.pallas_call(functools.partial(pack_kernel, n_ka, reps, sec), out_shape...  1.36 us
  transfers between devices with their start and end apart: 2, of which 0 were waited for; matrix products, arithmetic and copies ran while one was open for 0% of the time, Pallas kernels for 10%

profile of v3, /device:TPU:0, one launch (start us, length us, event | category | flops | bytes accessed | tf_op | source)
XLA Modules:
  0.0 45.0 jit_solution(17152374308363307368)
XLA Ops:
  0.6 1.4 %shard_map.104 = bf16[1600,128]{1,0:T(8,128)(2,1)S(1)} custom-call(bf16[32,1024]{1,0:T(8,128)(2,1)} %refs_0_.2, bf16[32,1024]{1,0:T(8,128)(2,1)} %refs_1_.2, bf16[2,32,1024]{2,1,0:T(8,128)(2,1)} %bitcast.11, bf16[2,32,1024]{2,1,0:T(8,128)(2,1)} %bitcast.12, bf16[16,32]{1,0:T(8,128)(2,1)} %refs_4_.1, bf16[16,32]{1,0:T(8,128)(2,1)} %refs_5_.1), custom_call_target="tpu_custom_call" | custom-call | tf_op jit(solution)/shard_map/pallas_call | solution.py:341
  2.0 20.7 %all_to_all.10 = bf16[32,25,2,128]{3,2,1,0:T(2,128)(2,1)S(1)} all-to-all(bf16[32,25,2,128]{3,2,1,0:T(2,128)(2,1)S(1)} %bitcast.8), channel_id=1, replica_groups=mesh['pb'=8,'ka'=4] {'pb','ka'}, dimensions={0} | all-to-all | bytes 819200 | tf_op jit(solution)/shard_map/all_to_all | solution.py:305
  22.7 0.1 shard_map.105.queries_ref
  22.8 0.0 collective-permute-start
  22.8 2.2 %shard_map.106 = (bf16[1024,128]{1,0:T(8,128)(2,1)S(1)}, bf16[64,1024]{1,0:T(8,128)(2,1)S(1)}, f32[1024,128]{1,0:T(8,128)S(1)}, bf16[2,64,256]{2,1,0:T(8,128)(2,...) custom-call(bf16[1600,128]{1,0:T(8,128)(2,1)S(1)} %bitcast.7, ...), custom_call_target="tpu_custom_call" | custom-call | flops 335544320 | bytes 1048576 | tf_op jit(solution)/shard_map/pallas_call | solution.py:365
  25.1 0.6 %collective-permute-start.1 = (bf16[2,64,256]{2,1,0:T(8,128)(2,1)S(1)}, bf16[2,64,256]{2,1,0:T(8,128)(2,1)S(1)}, u32[]{:S(2)}, u32[]{:S(2)}) collective-permute-start(bf16[2,64,256]{2,1,0:T(8,128)(2,1)S(1)} %get-tuple-element.16), channel_id=1, source_target_pairs={{0,1},{1,0},{2,3},{3,2},{4,5},{5,4},{6,7},{7,6},{8,9},{9,8},{10,11... | collective-permute-start | bytes 196616 | tf_op jit(solution)/shard_map/ppermute | solution.py:385
  25.6 0.0 collective-permute-done.queries_ref
  25.6 2.1 %shard_map.107 = (bf16[1024,128]{1,0:T(8,128)(2,1)S(1)}, f32[2,64,256]{2,1,0:T(8,128)S(1)}, bf16[1024,1024]{1,0:T(8,128)(2,1)S(1)}) custom-call(bf16[520,128]{1,0:T(8,128)(2,1)S(1)} %collective-permute-done.queries_ref, bf16[1024,128]{1,0:T(8,128)(2,1)S(1)} %get-tuple-element.11.kv_ref, bf16[64,1024]{1,0:T(8,128)(2,1)S(1)} %get-tuple-element.12.kt_ref, ...), custom_call_target="tpu_custom_call" | custom-call | flops 335544320 | bytes 1048576 | tf_op jit(solution)/shard_map/pallas_call | solution.py:386
  27.7 0.0 collective-permute-done.1.other_ref
  27.7 0.1 shard_map.108
  27.8 14.4 %all_to_all.11 = bf16[32,20,2,128]{3,2,1,0:T(2,128)(2,1)S(1)} all-to-all(bf16[32,20,2,128]{3,2,1,0:T(2,128)(2,1)S(1)} %bitcast.10), channel_id=1, replica_groups=mesh['pb'=8,'ka'=4] {'pb','ka'}, dimensions={0} | all-to-all | bytes 655360 | tf_op jit(solution)/shard_map/all_to_all | solution.py:305
  42.3 2.7 %shard_map.109 = (bf16[32,1024]{1,0:T(8,128)(2,1)}, bf16[64,1024]{1,0:T(8,128)(2,1)}) custom-call(bf16[1280,128]{1,0:T(8,128)(2,1)S(1)} %bitcast.9, bf16[1024,1024]{1,0:T(8,128)(2,1)S(1)} %get-tuple-element.17.wq_ref, bf16[1024,1024]{1,0:T(8,128)(2,1)S(1)} %get-tuple-element.18.wk_ref, bf16[1024,1024]{1,0:T(8,128)(2,1)S(1)} %get-tuple-element.19.wv_ref), custom_call_target="tpu_custom_call" | custom-call | tf_op jit(solution)/shard_map/pallas_call | solution.py:407
Async XLA Ops:
  22.8 2.9 %collective-permute-start = (bf16[520,128]{1,0:T(8,128)(2,1)S(1)}, bf16[520,128]{1,0:T(8,128)(2,1)S(1)}, u32[]{:S(2)}, u32[]{:S(2)}) collective-permute-start(bf16[520,128]{1,0:T(8,128)(2,1)S(1)} %shard_map.105.queries_ref), channel_id=1, source_target_pairs={{0,1},{1,0},{2,3},{3,2},{4,5},{5,4},{6,7},{7,6},{8,9},{9,8},{10,11... | collective-permute-start | bytes 399368 | tf_op jit(solution)/shard_map/ppermute | solution.py:359
  25.1 2.6 %collective-permute-start.1 = (bf16[2,64,256]{2,1,0:T(8,128)(2,1)S(1)}, bf16[2,64,256]{2,1,0:T(8,128)(2,1)S(1)}, u32[]{:S(2)}, u32[]{:S(2)}) collective-permute-start(bf16[2,64,256]{2,1,0:T(8,128)(2,1)S(1)} %get-tuple-element.16), channel_id=1, source_target_pairs={{0,1},{1,0},{2,3},{3,2},{4,5},{5,4},{6,7},{7,6},{8,9},{9,8},{10,11... | collective-permute-start | bytes 196616 | tf_op jit(solution)/shard_map/ppermute | solution.py:385

commit v4 on v3

--- a/solution.py
+++ b/solution.py
@@ -43,18 +43,22 @@
 
 def pack_kernel(n_ka, reps, sec, *refs):
     sources, out_ref, (*held, sems) = refs[:6], refs[6], refs[7:]
-    for copy in fetch(sources, held, sems):
-        copy.wait()
-    q_ref, g_ref, k_ref, v_ref, norm_ref, delta_ref = held
+    copies = fetch(sources, held, sems)
+    norm_ref, delta_ref, q_ref, g_ref, k_ref, v_ref = held
+
+    def arrive(*which):
+        for index in which:
+            copies[index].wait()
+
     heads, rows = norm_ref.shape
     kept = k_ref.shape[1]
     half = rows // 2
+    quarter = half // 2
     size = sec + half + 2
     me = lax.axis_index("pb") * n_ka + lax.axis_index("ka")
     slot = lax.rem(me, LANES // half)
     token = lax.broadcasted_iota(jnp.int32, (rows, 2 * LANES), 0)
     lane = lax.broadcasted_iota(jnp.int32, (rows, 2 * LANES), 1)
-    quarter = half // 2
     target = (
         lax.div(token, half) * LANES
         + lax.rem(lax.div(token, quarter), 2) * HEAD_DIM
@@ -62,6 +66,12 @@
         + lax.rem(token, quarter)
     )
     place = jnp.where(lane == target, 1.0, 0.0).astype(BF16)
+    row = lax.broadcasted_iota(jnp.int32, (heads * 4, heads * 4), 0)
+    col = lax.broadcasted_iota(jnp.int32, (heads * 4, heads * 4), 1)
+    inner = lax.rem(row, 4)
+    wanted = (lax.rem(inner, 2) * 2 + lax.div(inner, 2)) * heads + lax.div(row, 4)
+    pick = jnp.where(col == wanted, 1.0, 0.0).astype(BF16)
+    arrive(0, 1)
     both = jnp.concatenate([norm_ref[...], delta_ref[...]], axis=0)
     moved = jnp.dot(both, place, preferred_element_type=F32)
     stacked = jnp.concatenate(
@@ -73,34 +83,37 @@
         ],
         axis=0,
     ).astype(BF16)
-    row = lax.broadcasted_iota(jnp.int32, (heads * 4, heads * 4), 0)
-    col = lax.broadcasted_iota(jnp.int32, (heads * 4, heads * 4), 1)
-    inner = lax.rem(row, 4)
-    wanted = (lax.rem(inner, 2) * 2 + lax.div(inner, 2)) * heads + lax.div(row, 4)
-    pick = jnp.where(col == wanted, 1.0, 0.0).astype(BF16)
     extra = jnp.dot(pick, stacked, preferred_element_type=F32)
 
+    def chunks(pair):
+        for which in range(2):
+            for rep in range(reps):
+                head = 2 * pair + which
+                yield which, head, rep, (head * reps + rep) * size
+
+    arrive(2, 3)
     for pair in range(heads // 2):
         cols = slice(pair * LANES, (pair + 1) * LANES)
         queries = regroup(q_ref[:, cols].astype(F32), g_ref[:, cols].astype(F32))
+        for which, head, rep, base in chunks(pair):
+            side = rep % 2
+            out_ref[base + sec : base + sec + half, :] = queries[which][
+                side * half : (side + 1) * half
+            ].astype(BF16)
+            first = head * 4 + side * 2
+            out_ref[base + sec + half : base + size, :] = extra[first : first + 2].astype(BF16)
+    arrive(4, 5)
+    for pair in range(heads // 2):
+        cols = slice(pair * LANES, (pair + 1) * LANES)
         keys = [
             regroup(k_ref[rep, :, cols].astype(F32), v_ref[rep, :, cols].astype(F32))
             for rep in range(reps)
         ]
-        for which in range(2):
-            head = 2 * pair + which
-            for rep in range(reps):
-                base = (head * reps + rep) * size
-                side = rep % 2
-                key_rows = keys[rep][which]
-                if kept < sec:
-                    key_rows = jnp.concatenate([key_rows, jnp.zeros((sec - kept, LANES), F32)], axis=0)
-                out_ref[base : base + sec, :] = key_rows.astype(BF16)
-                out_ref[base + sec : base + sec + half, :] = queries[which][
-                    side * half : (side + 1) * half
-                ].astype(BF16)
-                first = head * 4 + side * 2
-                out_ref[base + sec + half : base + size, :] = extra[first : first + 2].astype(BF16)
+        for which, head, rep, base in chunks(pair):
+            key_rows = keys[rep][which]
+            if kept < sec:
+                key_rows = jnp.concatenate([key_rows, jnp.zeros((sec - kept, LANES), F32)], axis=0)
+            out_ref[base : base + sec, :] = key_rows.astype(BF16)
 
 
 def split_kernel(count, sec, half, in_ref, own_ref):
@@ -126,7 +139,7 @@
     own_ref[base : base + len(rows), :] = jnp.concatenate(rows, axis=0).astype(BF16)
 
 
-def attend(queries_ref, saved_ref, kv_ref, kt_ref, gq_ref, emit):
+def attend(queries_ref, saved_ref, probs_ref, scores_ref, kv_ref, kt_ref, gq_ref, emit):
     keys = kv_ref.shape[0]
     low = low_lanes(TILE)
     blocks = gq_ref.shape[0]
@@ -153,24 +166,25 @@
                 for kind in range(2)
             )
             sides.append((queries, grads, norm * LOG2E, delta))
-        totals = [None, None]
         for tile in range(keys // TILE):
             span = slice(tile * TILE, (tile + 1) * TILE)
             kv = kv_ref[span, :]
-            part = None
             for side, (queries, grads, norm, delta) in enumerate(sides):
+                cols = slice(side * TILE, (side + 1) * TILE)
                 scores = lax.dot_general(kv, queries, ROWS_BY_ROWS, preferred_element_type=F32)
                 grad_probs = lax.dot_general(kv, grads, ROWS_BY_ROWS, preferred_element_type=F32)
                 probs = jnp.exp2(scores * LOG2E - norm)
-                grad_scores = (probs * (grad_probs - delta)).astype(BF16)
-                first = jnp.dot(probs.astype(BF16), grads, preferred_element_type=F32)
-                part = first if part is None else part + first
-                part += jnp.dot(grad_scores, queries, preferred_element_type=F32)
-                more = jnp.dot(kt_ref[:, span], grad_scores, preferred_element_type=F32)
-                totals[side] = more if totals[side] is None else totals[side] + more
-            emit(span, part)
+                probs_ref[span, cols] = probs.astype(BF16)
+                scores_ref[span, cols] = (probs * (grad_probs - delta)).astype(BF16)
+        queries, grads = (jnp.concatenate([side[kind] for side in sides], axis=0) for kind in range(2))
+        grad_scores = scores_ref[...]
+        grad_query = jnp.dot(kt_ref[...], grad_scores, preferred_element_type=F32)
         for side in range(2):
-            gq_ref[2 * pair + side] = totals[side]
+            gq_ref[2 * pair + side] = grad_query[:, side * TILE : (side + 1) * TILE]
+        emit(
+            jnp.dot(probs_ref[...], grads, preferred_element_type=F32)
+            + jnp.dot(grad_scores, queries, preferred_element_type=F32)
+        )
 
     if blocks == 2:
         step(0)
@@ -179,13 +193,7 @@
 
 
 def own_kernel(count, sec, half, in_ref, queries_ref, *refs):
-    weights, (kv_ref, kt_ref, acc_ref, gqb_ref), near, (gq_ref, saved_ref, sems) = (
-        refs[:2],
-        refs[2:6],
-        refs[6:8],
-        refs[8:],
-    )
-    copies = fetch(weights, near, sems)
+    kv_ref, kt_ref, acc_ref, gqb_ref, gq_ref, *work = refs
     size = sec + half + 2
     per_tile = TILE // sec
     for tile in range(count * sec // TILE):
@@ -204,33 +212,28 @@
     if not once:
         acc_ref[...] = jnp.zeros_like(acc_ref)
 
-    def emit(span, part):
-        acc_ref[span, :] = part if once else acc_ref[span, :] + part
-
-    attend(queries_ref, saved_ref, kv_ref, kt_ref, gq_ref, emit)
+    def emit(part):
+        acc_ref[...] = part if once else acc_ref[...] + part
+
+    attend(queries_ref, *work, kv_ref, kt_ref, gq_ref, emit)
     gqb_ref[...] = gq_ref[...].astype(BF16)
-    for copy in copies:
-        copy.wait()
-
-
-def far_kernel(queries_ref, kv_ref, kt_ref, start_ref, weight_ref, *refs):
-    dkv_ref, gq_ref, near_ref, acc_ref, saved_ref, sems = refs
-    copies = fetch([weight_ref], [near_ref], sems)
+
+
+def far_kernel(queries_ref, kv_ref, kt_ref, start_ref, *refs):
+    dkv_ref, gq_ref, acc_ref, *work = refs
     once = gq_ref.shape[0] == 2
     if not once:
         acc_ref[...] = start_ref[...]
 
-    def emit(span, part):
+    def emit(part):
         if once:
-            dkv_ref[span, :] = (start_ref[span, :] + part).astype(BF16)
+            dkv_ref[...] = (start_ref[...] + part).astype(BF16)
         else:
-            acc_ref[span, :] += part
-
-    attend(queries_ref, saved_ref, kv_ref, kt_ref, gq_ref, emit)
+            acc_ref[...] += part
+
+    attend(queries_ref, *work, kv_ref, kt_ref, gq_ref, emit)
     if not once:
         dkv_ref[...] = acc_ref[...].astype(BF16)
-    for copy in copies:
-        copy.wait()
 
 
 def gather_kernel(count, sec, quarter, dkv_ref, gq_ref, other_ref, out_ref):
@@ -254,9 +257,8 @@
             ].astype(BF16)
 
 
-def project_kernel(
-    reps, sec, quarter, in_ref, wq_ref, wk_ref, wv_ref, dxq_ref, dxkv_ref, gq_ref, gk_ref, gv_ref
-):
+def project_kernel(reps, sec, quarter, in_ref, wq_ref, wk_ref, wv_ref, dxq_ref, dxkv_ref, *refs):
+    gq_ref, gk_ref, gv_ref, qs_ref, kvs_ref, sems = refs
     size = sec + quarter
     heads = in_ref.shape[0] // (reps * size)
     for pair in range(heads // 2):
@@ -279,13 +281,36 @@
                 first = (2 * side + part) * quarter
                 gq_ref[first : first + quarter, cols] = rows.astype(BF16)
 
-    def times(grads_ref, weight_ref):
+    def across(grads_ref, weight_ref, span):
         return lax.dot_general(
-            grads_ref[...], weight_ref[...], ROWS_BY_ROWS, preferred_element_type=F32
+            grads_ref[...], weight_ref[span, :], ROWS_BY_ROWS, preferred_element_type=F32
         )
 
-    dxq_ref[...] = times(gq_ref, wq_ref).astype(BF16)
-    dxkv_ref[...] = (times(gk_ref, wk_ref) + times(gv_ref, wv_ref)).astype(BF16)
+    def turned(grads_ref, weight_ref, span):
+        return lax.dot_general(
+            weight_ref[span, :], grads_ref[...], ROWS_BY_ROWS, preferred_element_type=F32
+        ).T
+
+    width = wq_ref.shape[0]
+    writes = []
+
+    def write(stage_ref, target_ref, span, value):
+        stage_ref[:, span] = value.astype(BF16)
+        copy = pltpu.make_async_copy(
+            stage_ref.at[:, span], target_ref.at[:, span], sems.at[len(writes)]
+        )
+        copy.start()
+        writes.append(copy)
+
+    step = width // 2
+    for first in range(0, width, step):
+        span = pl.ds(first, step)
+        value = across(gk_ref, wk_ref, span) + turned(gv_ref, wv_ref, span)
+        write(kvs_ref, dxkv_ref, span, value)
+    write(qs_ref, dxq_ref, pl.ds(0, step), across(gq_ref, wq_ref, pl.ds(0, step)))
+    write(qs_ref, dxq_ref, pl.ds(step, step), turned(gq_ref, wq_ref, pl.ds(step, step)))
+    for copy in writes:
+        copy.wait()
 
 
 def in_vmem(count):
@@ -331,12 +356,12 @@
         raise ValueError("sizes")
 
     inputs = [
+        log_norm,
+        row_delta,
         query_saved,
         out_grad,
         key_saved.reshape(reps, kept, width),
         value_saved.reshape(reps, kept, width),
-        log_norm,
-        row_delta,
     ]
     sent = pl.pallas_call(
         functools.partial(pack_kernel, n_ka, reps, sec),
@@ -358,44 +383,44 @@
     twins = [(index, index ^ 1) for index in range(count)]
     far = lax.ppermute(own, AXES, twins)
     work = pl.CostEstimate(
-        flops=10 * queries * keys * HEAD_DIM, transcendentals=queries * keys, bytes_accessed=1 << 20
+        flops=40 * queries * keys * HEAD_DIM, transcendentals=queries * keys, bytes_accessed=1 << 20
     )
     blocks = queries // TILE
-    saved = pltpu.VMEM((2 * queries // LANES, LANES), F32)
-    kv, kt, acc, own_part, near_key, near_value = pl.pallas_call(
+    scratch = [
+        pltpu.VMEM((2 * queries // LANES, LANES), F32),
+        pltpu.VMEM((keys, 2 * TILE), BF16),
+        pltpu.VMEM((keys, 2 * TILE), BF16),
+    ]
+    kv, kt, acc, own_part = pl.pallas_call(
         functools.partial(own_kernel, count, sec, half),
         out_shape=[
             pltpu.VMEM((keys, LANES), BF16),
             pltpu.VMEM((HEAD_DIM, keys), BF16),
             pltpu.VMEM((keys, LANES), F32),
             pltpu.VMEM((blocks, HEAD_DIM, TILE), BF16),
-            pltpu.VMEM(weight_key.shape, BF16),
-            pltpu.VMEM(weight_value.shape, BF16),
         ],
-        in_specs=in_vmem(2) + in_hbm(2),
-        out_specs=in_vmem(6),
+        in_specs=in_vmem(2),
+        out_specs=in_vmem(4),
         scratch_shapes=[
             pltpu.VMEM((blocks, HEAD_DIM, TILE), F32),
-            saved,
-            pltpu.SemaphoreType.DMA((2,)),
+            *scratch,
         ],
         compiler_params=PARAMS,
         cost_estimate=work,
-    )(held, own, *keep_in_hbm([weight_key, weight_value]))
+    )(held, own)
     other_part = lax.ppermute(own_part, AXES, twins)
-    grad_keyvalue, far_part, near_query = pl.pallas_call(
+    grad_keyvalue, far_part = pl.pallas_call(
         far_kernel,
         out_shape=[
             pltpu.VMEM((keys, LANES), BF16),
             pltpu.VMEM((blocks, HEAD_DIM, TILE), F32),
-            pltpu.VMEM(weight_query.shape, BF16),
         ],
-        in_specs=in_vmem(4) + in_hbm(1),
-        out_specs=in_vmem(3),
-        scratch_shapes=[pltpu.VMEM((keys, LANES), F32), saved, pltpu.SemaphoreType.DMA((1,))],
+        in_specs=in_vmem(4),
+        out_specs=in_vmem(2),
+        scratch_shapes=[pltpu.VMEM((keys, LANES), F32), *scratch],
         compiler_params=PARAMS,
         cost_estimate=work,
-    )(far, kv, kt, acc, *keep_in_hbm([weight_query]))
+    )(far, kv, kt, acc)
     grads = pl.pallas_call(
         functools.partial(gather_kernel, count, sec, half // 2),
         out_shape=pltpu.VMEM((count * (sec + half // 2), LANES), BF16),
@@ -411,14 +436,23 @@
             jax.ShapeDtypeStruct((reps * sec, width), BF16),
         ),
         in_specs=in_vmem(4),
-        out_specs=tuple(in_vmem(2)),
+        out_specs=tuple(in_hbm(2)),
         scratch_shapes=[
             pltpu.VMEM((rows, width), BF16),
             pltpu.VMEM((reps * sec, width), BF16),
             pltpu.VMEM((reps * sec, width), BF16),
+            pltpu.VMEM((rows, width), BF16),
+            pltpu.VMEM((reps * sec, width), BF16),
+            pltpu.SemaphoreType.DMA((4,)),
         ],
         compiler_params=PARAMS,
-    )(returned, near_query, near_key, near_value)
+    )(
+        returned,
+        *(
+            pltpu.with_memory_space_constraint(weight, pltpu.VMEM)
+            for weight in (weight_query, weight_key, weight_value)
+        ),
+    )
     if kept != sec:
         dx_keyvalue = dx_keyvalue.reshape(reps, sec, width)[:, :kept].reshape(key_rows, width)
     return dx_query, dx_keyvalue

time: 45.1 us -> 43.6 us (0.967)
  Pallas kernels: 8.56 us -> 6.97 us
    pallas_call x1, Pallas kernels: 2.24 us -> 1.45 us  [local(): pl.pallas_call(functools.partial(own_kernel, count, sec, half), out_shape...]
    pallas_call x1, Pallas kernels: 2.07 us -> 1.46 us  [local(): pl.pallas_call(far_kernel, out_shape=[pltpu.VMEM((keys, LANES), BF16), pl...]
  transfers between devices with their start and end apart: 2 -> 2, of which waited for: 0 -> 0; matrix products, arithmetic and copies ran while one was open for 0% -> 0% of each run, Pallas kernels for 10% -> 7%
where the time goes in v4:
time: 43.6 us; the launch traced here: 43.4 us
  blocking collectives  35.1 us (81%)
  Pallas kernels  6.97 us (16%)
  between operations  0.68 us (2%)
  starting transfers between devices  0.6 us (1%)
    all_to_all x2, blocking collectives, exchange(): return lax.all_to_all(chunks, AXES, 0, 0).reshape(packed.shape)  35.1 us
    pallas_call x1, Pallas kernels, local(): pl.pallas_call(functools.partial(project_kernel, reps, sec, half // 2), o...  2.58 us
    pallas_call x1, Pallas kernels, local(): pl.pallas_call(far_kernel, out_shape=[pltpu.VMEM((keys, LANES), BF16), pl...  1.46 us
    pallas_call x1, Pallas kernels, local(): pl.pallas_call(functools.partial(own_kernel, count, sec, half), out_shape...  1.45 us
    pallas_call x1, Pallas kernels, local(): pl.pallas_call(functools.partial(pack_kernel, n_ka, reps, sec), out_shape...  1.29 us
  transfers between devices with their start and end apart: 2, of which 0 were waited for; matrix products, arithmetic and copies ran while one was open for 0% of the time, Pallas kernels for 7%

profile of v4, /device:TPU:0, one launch (start us, length us, event | category | flops | bytes accessed | tf_op | source)
XLA Modules:
  0.0 43.4 jit_solution(11992835599863838767)
XLA Ops:
  0.6 1.3 %shard_map.104 = bf16[1600,128]{1,0:T(8,128)(2,1)S(1)} custom-call(bf16[16,32]{1,0:T(8,128)(2,1)} %refs_0_.1, bf16[16,32]{1,0:T(8,128)(2,1)} %refs_1_.1, bf16[32,1024]{1,0:T(8,128)(2,1)} %refs_2_.1, bf16[32,1024]{1,0:T(8,128)(2,1)} %refs_3_.1, bf16[2,32,1024]{2,1,0:T(8,128)(2,1)} %bitcast.11, bf16[2,32,1024]{2,1,0:T(8,128)(2,1)} %bitcast.12), custom_call_target="tpu_custom_call" | custom-call | tf_op jit(solution)/shard_map/pallas_call | solution.py:366
  1.9 20.7 %all_to_all.10 = bf16[32,25,2,128]{3,2,1,0:T(2,128)(2,1)S(1)} all-to-all(bf16[32,25,2,128]{3,2,1,0:T(2,128)(2,1)S(1)} %bitcast.8), channel_id=1, replica_groups=mesh['pb'=8,'ka'=4] {'pb','ka'}, dimensions={0} | all-to-all | bytes 819200 | tf_op jit(solution)/shard_map/all_to_all | solution.py:330
  22.6 0.1 shard_map.105.queries_ref
  22.7 0.0 collective-permute-start
  22.7 1.5 %shard_map.106 = (bf16[1024,128]{1,0:T(8,128)(2,1)S(1)}, bf16[64,1024]{1,0:T(8,128)(2,1)S(1)}, f32[1024,128]{1,0:T(8,128)S(1)}, bf16[2,64,256]{2,1,0:T(8,128)(2,1)S(1)}) custom-call(bf16[1600,128]{1,0:T(8,128)(2,1)S(1)} %bitcast.7, bf16[520,128]{1,0:T(8,128)(2,1)S(1)} %shard_map.105.queries_ref), custom_call_target="tpu_custom_call" | custom-call | flops 1342177280 | bytes 1048576 | tf_op jit(solution)/shard_map/pallas_call | solution.py:394
  24.2 0.6 %collective-permute-start.1 = (bf16[2,64,256]{2,1,0:T(8,128)(2,1)S(1)}, bf16[2,64,256]{2,1,0:T(8,128)(2,1)S(1)}, u32[]{:S(2)}, u32[]{:S(2)}) collective-permute-start(bf16[2,64,256]{2,1,0:T(8,128)(2,1)S(1)} %get-tuple-element.13), channel_id=1, source_target_pairs={{0,1},{1,0},{2,3},{3,2},{4,5},{5,4},{6,7},{7,6},{8,9},{9,8},{10,11... | collective-permute-start | bytes 196616 | tf_op jit(solution)/shard_map/ppermute | solution.py:411
  24.8 0.0 collective-permute-done.queries_ref
  24.8 0.0 copy-start
  24.8 0.0 copy-start.1
  24.8 0.0 copy-start.2
  24.8 1.5 %shard_map.107 = (bf16[1024,128]{1,0:T(8,128)(2,1)S(1)}, f32[2,64,256]{2,1,0:T(8,128)S(1)}) custom-call(bf16[520,128]{1,0:T(8,128)(2,1)S(1)} %collective-permute-done.queries_ref, bf16[1024,128]{1,0:T(8,128)(2,1)S(1)} %get-tuple-element.8.kv_ref, bf16[64,1024]{1,0:T(8,128)(2,1)S(1)} %get-tuple-element.9.kt_ref, f32[1024,128]{1,0:T(8,128)S(1)} %get-tuple-element.10.start_ref), custom_call_target="tpu_custom_call" | custom-call | flops 1342177280 | bytes 1048576 | tf_op jit(solution)/shard_map/pallas_call | solution.py:412
  26.2 0.0 collective-permute-done.1.other_ref
  26.2 0.1 shard_map.108
  26.4 14.4 %all_to_all.11 = bf16[32,20,2,128]{3,2,1,0:T(2,128)(2,1)S(1)} all-to-all(bf16[32,20,2,128]{3,2,1,0:T(2,128)(2,1)S(1)} %bitcast.10), channel_id=1, replica_groups=mesh['pb'=8,'ka'=4] {'pb','ka'}, dimensions={0} | all-to-all | bytes 655360 | tf_op jit(solution)/shard_map/all_to_all | solution.py:330
  40.8 0.0 copy-done
  40.8 0.0 copy-done.1
  40.8 0.0 copy-done.2
  40.8 2.6 %shard_map.109 = (bf16[32,1024]{1,0:T(8,128)(2,1)}, bf16[64,1024]{1,0:T(8,128)(2,1)}) custom-call(bf16[1280,128]{1,0:T(8,128)(2,1)S(1)} %bitcast.9, bf16[1024,1024]{1,0:T(8,128)(2,1)S(1)} %copy-done, bf16[1024,1024]{1,0:T(8,128)(2,1)S(1)} %copy-done.1, bf16[1024,1024]{1,0:T(8,128)(2,1)S(1)} %copy-done.2), custom_call_target="tpu_custom_call" | custom-call | tf_op jit(solution)/shard_map/pallas_call | solution.py:432
Async XLA Ops:
  22.7 2.1 %collective-permute-start = (bf16[520,128]{1,0:T(8,128)(2,1)S(1)}, bf16[520,128]{1,0:T(8,128)(2,1)S(1)}, u32[]{:S(2)}, u32[]{:S(2)}) collective-permute-start(bf16[520,128]{1,0:T(8,128)(2,1)S(1)} %shard_map.105.queries_ref), channel_id=1, source_target_pairs={{0,1},{1,0},{2,3},{3,2},{4,5},{5,4},{6,7},{7,6},{8,9},{9,8},{10,11... | collective-permute-start | bytes 399368 | tf_op jit(solution)/shard_map/ppermute | solution.py:384
  24.2 2.0 %collective-permute-start.1 = (bf16[2,64,256]{2,1,0:T(8,128)(2,1)S(1)}, bf16[2,64,256]{2,1,0:T(8,128)(2,1)S(1)}, u32[]{:S(2)}, u32[]{:S(2)}) collective-permute-start(bf16[2,64,256]{2,1,0:T(8,128)(2,1)S(1)} %get-tuple-element.13), channel_id=1, source_target_pairs={{0,1},{1,0},{2,3},{3,2},{4,5},{5,4},{6,7},{7,6},{8,9},{9,8},{10,11... | collective-permute-start | bytes 196616 | tf_op jit(solution)/shard_map/ppermute | solution.py:411
  24.8 16.0 %copy-start = (bf16[1024,1024]{1,0:T(8,128)(2,1)S(1)}, bf16[1024,1024]{1,0:T(8,128)(2,1)}, u32[]{:S(2)}) copy-start(bf16[1024,1024]{1,0:T(8,128)(2,1)} %wq_ref.1) | copy-start | bytes 6291460
  24.8 16.0 %copy-start.1 = (bf16[1024,1024]{1,0:T(8,128)(2,1)S(1)}, bf16[1024,1024]{1,0:T(8,128)(2,1)}, u32[]{:S(2)}) copy-start(bf16[1024,1024]{1,0:T(8,128)(2,1)} %wk_ref.1) | copy-start | bytes 6291460
  24.8 16.0 %copy-start.2 = (bf16[1024,1024]{1,0:T(8,128)(2,1)S(1)}, bf16[1024,1024]{1,0:T(8,128)(2,1)}, u32[]{:S(2)}) copy-start(bf16[1024,1024]{1,0:T(8,128)(2,1)} %wv_ref.1) | copy-start | bytes 6291460

commit v5 on v4

--- a/solution.py
+++ b/solution.py
@@ -177,14 +177,19 @@
                 probs_ref[span, cols] = probs.astype(BF16)
                 scores_ref[span, cols] = (probs * (grad_probs - delta)).astype(BF16)
         queries, grads = (jnp.concatenate([side[kind] for side in sides], axis=0) for kind in range(2))
-        grad_scores = scores_ref[...]
-        grad_query = jnp.dot(kt_ref[...], grad_scores, preferred_element_type=F32)
+        grad_query = None
+        for tile in range(keys // TILE):
+            span = slice(tile * TILE, (tile + 1) * TILE)
+            grad_scores = scores_ref[span, :]
+            more = jnp.dot(kt_ref[:, span], grad_scores, preferred_element_type=F32)
+            grad_query = more if grad_query is None else grad_query + more
+            emit(
+                span,
+                jnp.dot(probs_ref[span, :], grads, preferred_element_type=F32)
+                + jnp.dot(grad_scores, queries, preferred_element_type=F32),
+            )
         for side in range(2):
             gq_ref[2 * pair + side] = grad_query[:, side * TILE : (side + 1) * TILE]
-        emit(
-            jnp.dot(probs_ref[...], grads, preferred_element_type=F32)
-            + jnp.dot(grad_scores, queries, preferred_element_type=F32)
-        )
 
     if blocks == 2:
         step(0)
@@ -212,8 +217,8 @@
     if not once:
         acc_ref[...] = jnp.zeros_like(acc_ref)
 
-    def emit(part):
-        acc_ref[...] = part if once else acc_ref[...] + part
+    def emit(span, part):
+        acc_ref[span, :] = part if once else acc_ref[span, :] + part
 
     attend(queries_ref, *work, kv_ref, kt_ref, gq_ref, emit)
     gqb_ref[...] = gq_ref[...].astype(BF16)
@@ -225,11 +230,11 @@
     if not once:
         acc_ref[...] = start_ref[...]
 
-    def emit(part):
+    def emit(span, part):
         if once:
-            dkv_ref[...] = (start_ref[...] + part).astype(BF16)
+            dkv_ref[span, :] = (start_ref[span, :] + part).astype(BF16)
         else:
-            acc_ref[...] += part
+            acc_ref[span, :] += part
 
     attend(queries_ref, *work, kv_ref, kt_ref, gq_ref, emit)
     if not once:
@@ -303,12 +308,26 @@
         writes.append(copy)
 
     step = width // 2
+    depth = 2 * LANES
     for first in range(0, width, step):
         span = pl.ds(first, step)
-        value = across(gk_ref, wk_ref, span) + turned(gv_ref, wv_ref, span)
-        write(kvs_ref, dxkv_ref, span, value)
-    write(qs_ref, dxq_ref, pl.ds(0, step), across(gq_ref, wq_ref, pl.ds(0, step)))
-    write(qs_ref, dxq_ref, pl.ds(step, step), turned(gq_ref, wq_ref, pl.ds(step, step)))
+        left, right = None, None
+        for offset in range(0, width, depth):
+            cols = pl.ds(offset, depth)
+            more = lax.dot_general(gk_ref[:, cols], wk_ref[span, cols], ROWS_BY_ROWS, preferred_element_type=F32)
+            left = more if left is None else left + more
+            more = lax.dot_general(wv_ref[span, cols], gv_ref[:, cols], ROWS_BY_ROWS, preferred_element_type=F32)
+            right = more if right is None else right + more
+        write(kvs_ref, dxkv_ref, span, left + right.T)
+    left, right = None, None
+    for offset in range(0, width, depth):
+        cols = pl.ds(offset, depth)
+        more = lax.dot_general(gq_ref[:, cols], wq_ref[pl.ds(0, step), cols], ROWS_BY_ROWS, preferred_element_type=F32)
+        left = more if left is None else left + more
+        more = lax.dot_general(wq_ref[pl.ds(step, step), cols], gq_ref[:, cols], ROWS_BY_ROWS, preferred_element_type=F32)
+        right = more if right is None else right + more
+    write(qs_ref, dxq_ref, pl.ds(0, step), left)
+    write(qs_ref, dxq_ref, pl.ds(step, step), right.T)
     for copy in writes:
         copy.wait()
 

time: 43.6 us -> 43.2 us (level)
  transfers between devices with their start and end apart: 2 -> 2, of which waited for: 0 -> 0; matrix products, arithmetic and copies ran while one was open for 0% -> 0% of each run, Pallas kernels for 7% -> 6%
where the time goes in v5:
time: 43.2 us; the launch traced here: 43 us
  blocking collectives  35.1 us (81%)
  Pallas kernels  6.6 us (15%)
  between operations  0.69 us (2%)
  starting transfers between devices  0.6 us (1%)
    all_to_all x2, blocking collectives, exchange(): return lax.all_to_all(chunks, AXES, 0, 0).reshape(packed.shape)  35.1 us
    pallas_call x1, Pallas kernels, local(): pl.pallas_call(functools.partial(project_kernel, reps, sec, half // 2), o...  2.33 us
    pallas_call x1, Pallas kernels, local(): pl.pallas_call(functools.partial(own_kernel, count, sec, half), out_shape...  1.4 us
    pallas_call x1, Pallas kernels, local(): pl.pallas_call(far_kernel, out_shape=[pltpu.VMEM((keys, LANES), BF16), pl...  1.39 us
    pallas_call x1, Pallas kernels, local(): pl.pallas_call(functools.partial(pack_kernel, n_ka, reps, sec), out_shape...  1.29 us
  transfers between devices with their start and end apart: 2, of which 0 were waited for; matrix products, arithmetic and copies ran while one was open for 0% of the time, Pallas kernels for 6%

profile of v5, /device:TPU:0, one launch (start us, length us, event | category | flops | bytes accessed | tf_op | source)
XLA Modules:
  0.0 43.0 jit_solution(10998823585801087859)
XLA Ops:
  0.6 1.3 %shard_map.104 = bf16[1600,128]{1,0:T(8,128)(2,1)S(1)} custom-call(bf16[16,32]{1,0:T(8,128)(2,1)} %refs_0_.1, bf16[16,32]{1,0:T(8,128)(2,1)} %refs_1_.1, bf16[32,1024]{1,0:T(8,128)(2,1)} %refs_2_.1, bf16[32,1024]{1,0:T(8,128)(2,1)} %refs_3_.1, bf16[2,32,1024]{2,1,0:T(8,128)(2,1)} %bitcast.11, bf16[2,32,1024]{2,1,0:T(8,128)(2,1)} %bitcast.12), custom_call_target="tpu_custom_call" | custom-call | tf_op jit(solution)/shard_map/pallas_call | solution.py:385
  1.9 20.7 %all_to_all.10 = bf16[32,25,2,128]{3,2,1,0:T(2,128)(2,1)S(1)} all-to-all(bf16[32,25,2,128]{3,2,1,0:T(2,128)(2,1)S(1)} %bitcast.8), channel_id=1, replica_groups=mesh['pb'=8,'ka'=4] {'pb','ka'}, dimensions={0} | all-to-all | bytes 819200 | tf_op jit(solution)/shard_map/all_to_all | solution.py:349
  22.6 0.1 shard_map.105.queries_ref
  22.7 0.0 collective-permute-start
  22.7 1.4 %shard_map.106 = (bf16[1024,128]{1,0:T(8,128)(2,1)S(1)}, bf16[64,1024]{1,0:T(8,128)(2,1)S(1)}, f32[1024,128]{1,0:T(8,128)S(1)}, bf16[2,64,256]{2,1,0:T(8,128)(2,1)S(1)}) custom-call(bf16[1600,128]{1,0:T(8,128)(2,1)S(1)} %bitcast.7, bf16[520,128]{1,0:T(8,128)(2,1)S(1)} %shard_map.105.queries_ref), custom_call_target="tpu_custom_call" | custom-call | flops 1342177280 | bytes 1048576 | tf_op jit(solution)/shard_map/pallas_call | solution.py:413
  24.1 0.6 %collective-permute-start.1 = (bf16[2,64,256]{2,1,0:T(8,128)(2,1)S(1)}, bf16[2,64,256]{2,1,0:T(8,128)(2,1)S(1)}, u32[]{:S(2)}, u32[]{:S(2)}) collective-permute-start(bf16[2,64,256]{2,1,0:T(8,128)(2,1)S(1)} %get-tuple-element.13), channel_id=1, source_target_pairs={{0,1},{1,0},{2,3},{3,2},{4,5},{5,4},{6,7},{7,6},{8,9},{9,8},{10,11... | collective-permute-start | bytes 196616 | tf_op jit(solution)/shard_map/ppermute | solution.py:430
  24.7 0.0 collective-permute-done.queries_ref
  24.7 0.0 copy-start
  24.7 0.0 copy-start.1
  24.7 0.0 copy-start.2
  24.7 1.4 %shard_map.107 = (bf16[1024,128]{1,0:T(8,128)(2,1)S(1)}, f32[2,64,256]{2,1,0:T(8,128)S(1)}) custom-call(bf16[520,128]{1,0:T(8,128)(2,1)S(1)} %collective-permute-done.queries_ref, bf16[1024,128]{1,0:T(8,128)(2,1)S(1)} %get-tuple-element.8.kv_ref, bf16[64,1024]{1,0:T(8,128)(2,1)S(1)} %get-tuple-element.9.kt_ref, f32[1024,128]{1,0:T(8,128)S(1)} %get-tuple-element.10.start_ref), custom_call_target="tpu_custom_call" | custom-call | flops 1342177280 | bytes 1048576 | tf_op jit(solution)/shard_map/pallas_call | solution.py:431
  26.1 0.0 collective-permute-done.1.other_ref
  26.1 0.1 shard_map.108
  26.2 14.4 %all_to_all.11 = bf16[32,20,2,128]{3,2,1,0:T(2,128)(2,1)S(1)} all-to-all(bf16[32,20,2,128]{3,2,1,0:T(2,128)(2,1)S(1)} %bitcast.10), channel_id=1, replica_groups=mesh['pb'=8,'ka'=4] {'pb','ka'}, dimensions={0} | all-to-all | bytes 655360 | tf_op jit(solution)/shard_map/all_to_all | solution.py:349
  40.7 0.0 copy-done
  40.7 0.0 copy-done.1
  40.7 0.0 copy-done.2
  40.7 2.3 %shard_map.109 = (bf16[32,1024]{1,0:T(8,128)(2,1)}, bf16[64,1024]{1,0:T(8,128)(2,1)}) custom-call(bf16[1280,128]{1,0:T(8,128)(2,1)S(1)} %bitcast.9, bf16[1024,1024]{1,0:T(8,128)(2,1)S(1)} %copy-done, bf16[1024,1024]{1,0:T(8,128)(2,1)S(1)} %copy-done.1, bf16[1024,1024]{1,0:T(8,128)(2,1)S(1)} %copy-done.2), custom_call_target="tpu_custom_call" | custom-call | tf_op jit(solution)/shard_map/pallas_call | solution.py:451
Async XLA Ops:
  22.7 2.0 %collective-permute-start = (bf16[520,128]{1,0:T(8,128)(2,1)S(1)}, bf16[520,128]{1,0:T(8,128)(2,1)S(1)}, u32[]{:S(2)}, u32[]{:S(2)}) collective-permute-start(bf16[520,128]{1,0:T(8,128)(2,1)S(1)} %shard_map.105.queries_ref), channel_id=1, source_target_pairs={{0,1},{1,0},{2,3},{3,2},{4,5},{5,4},{6,7},{7,6},{8,9},{9,8},{10,11... | collective-permute-start | bytes 399368 | tf_op jit(solution)/shard_map/ppermute | solution.py:403
  24.1 2.0 %collective-permute-start.1 = (bf16[2,64,256]{2,1,0:T(8,128)(2,1)S(1)}, bf16[2,64,256]{2,1,0:T(8,128)(2,1)S(1)}, u32[]{:S(2)}, u32[]{:S(2)}) collective-permute-start(bf16[2,64,256]{2,1,0:T(8,128)(2,1)S(1)} %get-tuple-element.13), channel_id=1, source_target_pairs={{0,1},{1,0},{2,3},{3,2},{4,5},{5,4},{6,7},{7,6},{8,9},{9,8},{10,11... | collective-permute-start | bytes 196616 | tf_op jit(solution)/shard_map/ppermute | solution.py:430
  24.7 16.0 %copy-start = (bf16[1024,1024]{1,0:T(8,128)(2,1)S(1)}, bf16[1024,1024]{1,0:T(8,128)(2,1)}, u32[]{:S(2)}) copy-start(bf16[1024,1024]{1,0:T(8,128)(2,1)} %wq_ref.1) | copy-start | bytes 6291460
  24.7 16.0 %copy-start.1 = (bf16[1024,1024]{1,0:T(8,128)(2,1)S(1)}, bf16[1024,1024]{1,0:T(8,128)(2,1)}, u32[]{:S(2)}) copy-start(bf16[1024,1024]{1,0:T(8,128)(2,1)} %wk_ref.1) | copy-start | bytes 6291460
  24.7 16.0 %copy-start.2 = (bf16[1024,1024]{1,0:T(8,128)(2,1)S(1)}, bf16[1024,1024]{1,0:T(8,128)(2,1)}, u32[]{:S(2)}) copy-start(bf16[1024,1024]{1,0:T(8,128)(2,1)} %wv_ref.1) | copy-start | bytes 6291460

commit v6 on v5

--- a/solution.py
+++ b/solution.py
@@ -6,6 +6,7 @@
 from jax import lax
 from jax.experimental import pallas as pl
 from jax.experimental.pallas import tpu as pltpu
+from jax.sharding import Mesh
 from jax.sharding import PartitionSpec as P
 
 HEAD_DIM = 64
@@ -15,10 +16,17 @@
 TILE = 256
 VMEM_LIMIT = 24 * 1024 * 1024
 PARAMS = pltpu.CompilerParams(vmem_limit_bytes=VMEM_LIMIT)
-AXES = ("pb", "ka")
+PARTS = ("pb_hi", "pb_lo", "ka_hi", "ka_lo")
+AXES = ("pb_lo", "ka_hi", "ka_lo", "pb_hi")
 F32 = jnp.float32
 BF16 = jnp.bfloat16
 ROWS_BY_ROWS = (((1,), (1,)), ((), ()))
+
+
+def place_of(head, rep, reps, depth):
+    index = head * reps + rep
+    rest, twin = index // 2, index % 2
+    return (rest // depth * 2 + twin) * depth + rest % depth
 
 
 def low_lanes(rows):
@@ -41,7 +49,7 @@
     return copies
 
 
-def pack_kernel(n_ka, reps, sec, *refs):
+def pack_kernel(sizes, reps, sec, *refs):
     sources, out_ref, (*held, sems) = refs[:6], refs[6], refs[7:]
     copies = fetch(sources, held, sems)
     norm_ref, delta_ref, q_ref, g_ref, k_ref, v_ref = held
@@ -55,7 +63,10 @@
     half = rows // 2
     quarter = half // 2
     size = sec + half + 2
-    me = lax.axis_index("pb") * n_ka + lax.axis_index("ka")
+    depth = sizes["pb_hi"]
+    me = 0
+    for axis in AXES:
+        me = me * sizes[axis] + lax.axis_index(axis)
     slot = lax.rem(me, LANES // half)
     token = lax.broadcasted_iota(jnp.int32, (rows, 2 * LANES), 0)
     lane = lax.broadcasted_iota(jnp.int32, (rows, 2 * LANES), 1)
@@ -89,7 +100,7 @@
         for which in range(2):
             for rep in range(reps):
                 head = 2 * pair + which
-                yield which, head, rep, (head * reps + rep) * size
+                yield which, head, rep, place_of(head, rep, reps, depth) * size
 
     arrive(2, 3)
     for pair in range(heads // 2):
@@ -262,7 +273,7 @@
             ].astype(BF16)
 
 
-def project_kernel(reps, sec, quarter, in_ref, wq_ref, wk_ref, wv_ref, dxq_ref, dxkv_ref, *refs):
+def project_kernel(depth, reps, sec, quarter, in_ref, wq_ref, wk_ref, wv_ref, dxq_ref, dxkv_ref, *refs):
     gq_ref, gk_ref, gv_ref, qs_ref, kvs_ref, sems = refs
     size = sec + quarter
     heads = in_ref.shape[0] // (reps * size)
@@ -270,7 +281,9 @@
         cols = slice(pair * LANES, (pair + 1) * LANES)
         totals = [[None, None], [None, None]]
         for rep in range(reps):
-            bases = [((2 * pair + which) * reps + rep) * size for which in range(2)]
+            bases = [
+                place_of(2 * pair + which, rep, reps, depth) * size for which in range(2)
+            ]
             even, odd = (in_ref[base : base + sec, :].astype(F32) for base in bases)
             grad_key, grad_value = regroup(even, odd)
             span = slice(rep * sec, (rep + 1) * sec)
@@ -350,7 +363,7 @@
 
 
 def local(
-    n_ka,
+    sizes,
     count,
     query_saved,
     key_saved,
@@ -383,7 +396,7 @@
         value_saved.reshape(reps, kept, width),
     ]
     sent = pl.pallas_call(
-        functools.partial(pack_kernel, n_ka, reps, sec),
+        functools.partial(pack_kernel, sizes, reps, sec),
         out_shape=pltpu.VMEM((count * (sec + half + 2), LANES), BF16),
         in_specs=in_hbm(6),
         out_specs=in_vmem(1)[0],
@@ -399,8 +412,8 @@
         out_specs=in_vmem(1)[0],
         compiler_params=PARAMS,
     )(held)
-    twins = [(index, index ^ 1) for index in range(count)]
-    far = lax.ppermute(own, AXES, twins)
+    twins = [(0, 1), (1, 0)]
+    far = lax.ppermute(own, "ka_lo", twins)
     work = pl.CostEstimate(
         flops=40 * queries * keys * HEAD_DIM, transcendentals=queries * keys, bytes_accessed=1 << 20
     )
@@ -427,7 +440,7 @@
         compiler_params=PARAMS,
         cost_estimate=work,
     )(held, own)
-    other_part = lax.ppermute(own_part, AXES, twins)
+    other_part = lax.ppermute(own_part, "ka_lo", twins)
     grad_keyvalue, far_part = pl.pallas_call(
         far_kernel,
         out_shape=[
@@ -449,7 +462,7 @@
     )(grad_keyvalue, far_part, other_part)
     returned = exchange(grads, count)
     dx_query, dx_keyvalue = pl.pallas_call(
-        functools.partial(project_kernel, reps, sec, half // 2),
+        functools.partial(project_kernel, sizes["pb_hi"], reps, sec, half // 2),
         out_shape=(
             jax.ShapeDtypeStruct((rows, width), BF16),
             jax.ShapeDtypeStruct((reps * sec, width), BF16),
@@ -478,23 +491,25 @@
 
 
 def solution(mesh):
-    n_ka = mesh.shape["ka"]
-    count = mesh.shape["pb"] * n_ka
+    n_pb, n_ka = mesh.shape["pb"], mesh.shape["ka"]
+    sizes = dict(zip(PARTS, (n_pb // 2, 2, n_ka // 2, 2)))
+    split = Mesh(mesh.devices.reshape(tuple(sizes.values())), PARTS)
+    pb, ka = PARTS[:2], PARTS[2:]
     in_specs = (
-        P(("pb", "ka"), None),
-        P(("ka", "pb"), None),
-        P(("ka", "pb"), None),
-        P(("pb", "ka"), None),
-        P(None, ("pb", "ka")),
-        P(None, ("pb", "ka")),
+        P(pb + ka, None),
+        P(ka + pb, None),
+        P(ka + pb, None),
+        P(pb + ka, None),
+        P(None, pb + ka),
+        P(None, pb + ka),
         P(),
         P(),
         P(),
     )
-    out_specs = (P(("pb", "ka"), None), P(("ka", "pb"), None))
+    out_specs = (P(pb + ka, None), P(ka + pb, None))
     return jax.shard_map(
-        functools.partial(local, n_ka, count),
-        mesh=mesh,
+        functools.partial(local, sizes, n_pb * n_ka),
+        mesh=split,
         in_specs=in_specs,
         out_specs=out_specs,
         check_vma=False,

time: 43.2 us -> 42.4 us (0.981)
  blocking collectives: 35.1 us -> 33.2 us
  starting transfers between devices: 0.6 us -> 1.35 us
    all_to_all x2, blocking collectives: 35.1 us -> 33.2 us  [exchange(): return lax.all_to_all(chunks, AXES, 0, 0).reshape(packed.shape)]
    ppermute x2, starting transfers between devices: 0.6 us -> 1.35 us  [the longest x1 1.27 us: local(): far = lax.ppermute(own, 'ka_lo', twins)]
  transfers between devices with their start and end apart: 2 -> 2, of which waited for: 0 -> 0; matrix products, arithmetic and copies ran while one was open for 0% -> 0% of each run, Pallas kernels for 6% -> 7%
where the time goes in v6:
time: 42.4 us; the launch traced here: 41.9 us
  blocking collectives  33.2 us (78%)
  Pallas kernels  6.6 us (16%)
  starting transfers between devices  1.35 us (3%)
  between operations  0.7 us (2%)
    all_to_all x2, blocking collectives, exchange(): return lax.all_to_all(chunks, AXES, 0, 0).reshape(packed.shape)  33.2 us
    pallas_call x1, Pallas kernels, local(): pl.pallas_call(functools.partial(project_kernel, sizes['pb_hi'], reps, se...  2.33 us
    pallas_call x1, Pallas kernels, local(): pl.pallas_call(functools.partial(own_kernel, count, sec, half), out_shape...  1.4 us
    pallas_call x1, Pallas kernels, local(): pl.pallas_call(far_kernel, out_shape=[pltpu.VMEM((keys, LANES), BF16), pl...  1.38 us
    pallas_call x1, Pallas kernels, local(): pl.pallas_call(functools.partial(pack_kernel, sizes, reps, sec), out_shap...  1.29 us
    ppermute x1, starting transfers between devices, local(): far = lax.ppermute(own, 'ka_lo', twins)  1.27 us
  transfers between devices with their start and end apart: 2, of which 0 were waited for; matrix products, arithmetic and copies ran while one was open for 0% of the time, Pallas kernels for 7%

profile of v6, /device:TPU:0, one launch (start us, length us, event | category | flops | bytes accessed | tf_op | source)
XLA Modules:
  0.0 41.9 jit_solution(8977080823511612233)
XLA Ops:
  0.6 1.3 %shard_map.104 = bf16[1600,128]{1,0:T(8,128)(2,1)S(1)} custom-call(bf16[16,32]{1,0:T(8,128)(2,1)} %refs_0_.1, bf16[16,32]{1,0:T(8,128)(2,1)} %refs_1_.1, bf16[32,1024]{1,0:T(8,128)(2,1)} %refs_2_.1, bf16[32,1024]{1,0:T(8,128)(2,1)} %refs_3_.1, bf16[2,32,1024]{2,1,0:T(8,128)(2,1)} %bitcast.11, bf16[2,32,1024]{2,1,0:T(8,128)(2,1)} %bitcast.12), custom_call_target="tpu_custom_call" | custom-call | tf_op jit(solution)/shard_map/pallas_call | solution.py:398
  1.9 19.3 %all_to_all.10 = bf16[32,25,2,128]{3,2,1,0:T(2,128)(2,1)S(1)} all-to-all(bf16[32,25,2,128]{3,2,1,0:T(2,128)(2,1)S(1)} %bitcast.8), channel_id=1, replica_groups=mesh['pb_hi'=4,'pb_lo'=2,'ka_hi'=2,'ka_lo'=2] {'pb_lo','ka_hi','ka_lo','..., dimensions={0} | all-to-all | bytes 819200 | tf_op jit(solution)/shard_map/all_to_all | solution.py:362
  21.2 0.1 shard_map.105.queries_ref
  21.3 1.3 %collective-permute-start = (bf16[520,128]{1,0:T(8,128)(2,1)S(1)}, bf16[520,128]{1,0:T(8,128)(2,1)S(1)}, u32[]{:S(2)}, u32[]{:S(2)}) collective-permute-start(bf16[520,128]{1,0:T(8,128)(2,1)S(1)} %shard_map.105.queries_ref), channel_id=1, source_target_pairs={{0,1},{1,0},{2,3},{3,2},{4,5},{5,4},{6,7},{7,6},{8,9},{9,8},{10,11... | collective-permute-start | bytes 399368 | tf_op jit(solution)/shard_map/ppermute | solution.py:416
  22.6 1.4 %shard_map.106 = (bf16[1024,128]{1,0:T(8,128)(2,1)S(1)}, bf16[64,1024]{1,0:T(8,128)(2,1)S(1)}, f32[1024,128]{1,0:T(8,128)S(1)}, bf16[2,64,256]{2,1,0:T(8,128)(2,1)S(1)}) custom-call(bf16[1600,128]{1,0:T(8,128)(2,1)S(1)} %bitcast.7, bf16[520,128]{1,0:T(8,128)(2,1)S(1)} %shard_map.105.queries_ref), custom_call_target="tpu_custom_call" | custom-call | flops 1342177280 | bytes 1048576 | tf_op jit(solution)/shard_map/pallas_call | solution.py:426
  24.0 0.1 collective-permute-start.1
  24.0 0.0 collective-permute-done.queries_ref
  24.1 0.0 copy-start
  24.1 0.0 copy-start.1
  24.1 0.0 copy-start.2
  24.1 1.4 %shard_map.107 = (bf16[1024,128]{1,0:T(8,128)(2,1)S(1)}, f32[2,64,256]{2,1,0:T(8,128)S(1)}) custom-call(bf16[520,128]{1,0:T(8,128)(2,1)S(1)} %collective-permute-done.queries_ref, bf16[1024,128]{1,0:T(8,128)(2,1)S(1)} %get-tuple-element.8.kv_ref, bf16[64,1024]{1,0:T(8,128)(2,1)S(1)} %get-tuple-element.9.kt_ref, f32[1024,128]{1,0:T(8,128)S(1)} %get-tuple-element.10.start_ref), custom_call_target="tpu_custom_call" | custom-call | flops 1342177280 | bytes 1048576 | tf_op jit(solution)/shard_map/pallas_call | solution.py:444
  25.5 0.0 collective-permute-done.1.other_ref
  25.5 0.1 shard_map.108
  25.6 14.0 %all_to_all.11 = bf16[32,20,2,128]{3,2,1,0:T(2,128)(2,1)S(1)} all-to-all(bf16[32,20,2,128]{3,2,1,0:T(2,128)(2,1)S(1)} %bitcast.10), channel_id=1, replica_groups=mesh['pb_hi'=4,'pb_lo'=2,'ka_hi'=2,'ka_lo'=2] {'pb_lo','ka_hi','ka_lo','..., dimensions={0} | all-to-all | bytes 655360 | tf_op jit(solution)/shard_map/all_to_all | solution.py:362
  39.6 0.0 copy-done
  39.6 0.0 copy-done.1
  39.6 0.0 copy-done.2
  39.6 2.3 %shard_map.109 = (bf16[32,1024]{1,0:T(8,128)(2,1)}, bf16[64,1024]{1,0:T(8,128)(2,1)}) custom-call(bf16[1280,128]{1,0:T(8,128)(2,1)S(1)} %bitcast.9, bf16[1024,1024]{1,0:T(8,128)(2,1)S(1)} %copy-done, bf16[1024,1024]{1,0:T(8,128)(2,1)S(1)} %copy-done.1, bf16[1024,1024]{1,0:T(8,128)(2,1)S(1)} %copy-done.2), custom_call_target="tpu_custom_call" | custom-call | tf_op jit(solution)/shard_map/pallas_call | solution.py:464
Async XLA Ops:
  21.3 2.8 %collective-permute-start = (bf16[520,128]{1,0:T(8,128)(2,1)S(1)}, bf16[520,128]{1,0:T(8,128)(2,1)S(1)}, u32[]{:S(2)}, u32[]{:S(2)}) collective-permute-start(bf16[520,128]{1,0:T(8,128)(2,1)S(1)} %shard_map.105.queries_ref), channel_id=1, source_target_pairs={{0,1},{1,0},{2,3},{3,2},{4,5},{5,4},{6,7},{7,6},{8,9},{9,8},{10,11... | collective-permute-start | bytes 399368 | tf_op jit(solution)/shard_map/ppermute | solution.py:416
  24.0 1.5 %collective-permute-start.1 = (bf16[2,64,256]{2,1,0:T(8,128)(2,1)S(1)}, bf16[2,64,256]{2,1,0:T(8,128)(2,1)S(1)}, u32[]{:S(2)}, u32[]{:S(2)}) collective-permute-start(bf16[2,64,256]{2,1,0:T(8,128)(2,1)S(1)} %get-tuple-element.13), channel_id=1, source_target_pairs={{0,1},{1,0},{2,3},{3,2},{4,5},{5,4},{6,7},{7,6},{8,9},{9,8},{10,11... | collective-permute-start | bytes 196616 | tf_op jit(solution)/shard_map/ppermute | solution.py:443
  24.1 15.5 %copy-start = (bf16[1024,1024]{1,0:T(8,128)(2,1)S(1)}, bf16[1024,1024]{1,0:T(8,128)(2,1)}, u32[]{:S(2)}) copy-start(bf16[1024,1024]{1,0:T(8,128)(2,1)} %wq_ref.1) | copy-start | bytes 6291460
  24.1 15.5 %copy-start.1 = (bf16[1024,1024]{1,0:T(8,128)(2,1)S(1)}, bf16[1024,1024]{1,0:T(8,128)(2,1)}, u32[]{:S(2)}) copy-start(bf16[1024,1024]{1,0:T(8,128)(2,1)} %wk_ref.1) | copy-start | bytes 6291460
  24.1 15.5 %copy-start.2 = (bf16[1024,1024]{1,0:T(8,128)(2,1)S(1)}, bf16[1024,1024]{1,0:T(8,128)(2,1)}, u32[]{:S(2)}) copy-start(bf16[1024,1024]{1,0:T(8,128)(2,1)} %wv_ref.1) | copy-start | bytes 6291460
